TPU v7x, 32 devices: a whole 2x2x4 slice. The times are simulated.
32 devices in a mesh: tm: 1, space: 32 (over z, y, x, core).
Axes of the slice: x: 2, y: 2, z: 4, core: 2. Of those that a mesh axis runs over, the one named last changes fastest.
Arguments:
- links: float32 [8, 3, 2, 3, 2, 110592], P('tm', None, None, None, None, 'space'), may hold values from -1 to 1, as said below
Outputs:
- new_links: float32 [8, 3, 2, 3, 2, 110592], P('tm', None, None, None, None, 'space')
- theta: float32 [], replicated
- deficit: float32 [8], P('tm')
Inputs may be any that keep to these rules, and one draw needn't show every extreme that they name: `links`: each link's two stored rows are orthonormal complex 3-vectors, the first two rows of a special unitary matrix.
All inputs are finite; a program needn't handle non-finite values.
Results may differ from a plain program's by a relative error of at most 0.00013.
Values sent between devices are 32-bit elements; how exact they have to be, the bound alone decides.
A program may use at most 128 MiB of HBM per device.

v0:
```python
import functools
import math

import jax
import jax.numpy as jnp
import numpy as np
from jax import lax
from jax.experimental import pallas as pl
from jax.experimental.pallas import tpu as pltpu
from jax.sharding import PartitionSpec as P

EXTENT = 48
LANES = 128
HALF = 64
SEG = 16

root_three = math.sqrt(3.0)
step_size = 0.08
top_momentum = 12.0

f32 = jnp.float32
bf16 = jnp.bfloat16
MESH = pl.DeviceIdType.MESH
VM = pl.BlockSpec(memory_space=pltpu.VMEM)
PARAMS = pltpu.CompilerParams(vmem_limit_bytes=60 * 1024 * 1024)


def cmul(p, q):
    return (p[0] * q[0] - p[1] * q[1], p[0] * q[1] + p[1] * q[0])


def cadd(p, q):
    return (p[0] + q[0], p[1] + q[1])


def csub(p, q):
    return (p[0] - q[0], p[1] - q[1])


def conj(p):
    return (p[0], -p[1])


def conj_mul(p, q):
    return (p[0] * q[0] + p[1] * q[1], p[0] * q[1] - p[1] * q[0])


def mul_conj(p, q):
    return (p[0] * q[0] + p[1] * q[1], p[1] * q[0] - p[0] * q[1])


def dot_row(row, col, mul):
    out = mul(row[0], col[0])
    for k in (1, 2):
        out = cadd(out, mul(row[k], col[k]))
    return out


def cross_conj(a, b):
    return [
        conj(csub(cmul(a[(k + 1) % 3], b[(k + 2) % 3]), cmul(a[(k + 2) % 3], b[(k + 1) % 3])))
        for k in range(3)
    ]


def algebra_of(u):
    return [
        u[0][1][1] + u[1][0][1],
        u[0][1][0] - u[1][0][0],
        u[0][0][1] - u[1][1][1],
        u[0][2][1] + u[2][0][1],
        u[0][2][0] - u[2][0][0],
        u[1][2][1] + u[2][1][1],
        u[1][2][0] - u[2][1][0],
        (u[0][0][1] + u[1][1][1] - 2.0 * u[2][2][1]) * (1.0 / root_three),
    ]


def rotation_of(s):
    h = 0.5 * step_size
    s = [v * h for v in s]
    third = s[7] * (1.0 / root_three)
    d0, d1, d2 = s[2] + third, third - s[2], -2.0 * third
    herm = [
        [(d0, None), (s[0], -s[1]), (s[3], -s[4])],
        [(s[0], s[1]), (d1, None), (s[5], -s[6])],
        [(s[3], s[4]), (s[5], s[6]), (d2, None)],
    ]

    def mul(p, q):
        if p[1] is None and q[1] is None:
            return (p[0] * q[0], jnp.zeros_like(p[0]))
        if p[1] is None:
            return (p[0] * q[0], p[0] * q[1])
        if q[1] is None:
            return (p[0] * q[0], p[1] * q[0])
        return cmul(p, q)

    rows = []
    for i in range(2):
        row = []
        for j in range(3):
            sq = dot_row(herm[i], [herm[k][j] for k in range(3)], mul)
            re, im = -0.5 * sq[0], -0.5 * sq[1]
            if herm[i][j][1] is not None:
                re = re - herm[i][j][1]
            else:
                re = re + 1.0
            row.append((re, im + herm[i][j][0]))
        rows.append(row)

    def unit(row):
        inv = lax.rsqrt(sum(p[0] * p[0] + p[1] * p[1] for p in row))
        return [(p[0] * inv, p[1] * inv) for p in row]

    one = unit(rows[0])
    corr = dot_row(one, rows[1], conj_mul)
    two = unit([csub(rows[1][k], cmul(corr, one[k])) for k in range(3)])
    return [one, two, cross_conj(one, two)]


def block(k):
    return pl.ds(pl.multiple_of(k * LANES, LANES), LANES)


def lane_ids(rows=8):
    return lax.broadcasted_iota(jnp.int32, (rows, LANES), 1)


def load_link(ref, d, sl):
    rows = [[(ref[d, r, c, 0, :, sl], ref[d, r, c, 1, :, sl]) for c in range(3)] for r in range(2)]
    return rows + [cross_conj(rows[0], rows[1])]


def algebra_kernel(links, out):
    def step(k, carry):
        sl = block(k)
        for d in range(3):
            for a, v in enumerate(algebra_of(load_link(links, d, sl))):
                out[d, a, :, sl] = v
        return carry

    lax.fori_loop(0, links.shape[-1] // LANES, step, 0)


def split3(x):
    hi = x.astype(bf16)
    lo = (x - hi.astype(f32)).astype(bf16)
    return jnp.concatenate([hi, lo, hi], axis=0)


def transform(table, parts, sign):
    n = parts[0].shape[0]
    both = jnp.dot(table, split3(jnp.concatenate(parts, axis=1)), preferred_element_type=f32)
    outs = []
    for i in range(len(parts)):
        mine = both[:, i * LANES : (i + 1) * LANES]
        swapped = pltpu.roll(mine[n:], HALF, 1)
        outs.append(mine[:n] + jnp.where(lane_ids(n) < HALF, sign, -sign) * swapped)
    return outs


def packed_rows(q, count):
    free = HALF // SEG - count
    moved = -(-q * free // (count + free)) // 8 * 8
    return q - moved if free == 1 else q


def pack_rows(full, count):
    q = full.shape[0]
    kept = packed_rows(q, count)
    step = q - kept
    if step == 0:
        return full
    seg = lax.rem(lane_ids(step), HALF) // SEG
    pieces = []
    for m in range(count):
        moved = pltpu.roll(full[kept:], (count - m) * SEG, 1)
        pieces.append(jnp.where(seg == count, moved, full[m * step : (m + 1) * step]))
    return jnp.concatenate(pieces + [full[count * step : kept]], axis=0)


def unpack_rows(block_in, q, count):
    kept = block_in.shape[0]
    step = q - kept
    if step == 0:
        return block_in
    seg = lax.rem(lane_ids(step), HALF) // SEG
    tail = jnp.zeros((step, LANES), f32)
    for m in range(count):
        moved = pltpu.roll(block_in[m * step : (m + 1) * step], LANES - (count - m) * SEG, 1)
        tail = jnp.where(seg == m, moved, tail)
    return jnp.concatenate([block_in, tail], axis=0)


def spread_kernel(extent, head, nsplit, q, alg, y_rim, z_below, z_above, coords, table, out, theta, mat, rows, freq):
    nb = alg.shape[-1] // LANES
    yb = y_rim.shape[-1] // LANES
    qh = head // extent
    hb = head // LANES
    lane = lane_ids()
    mat[...] = jnp.zeros_like(mat)

    def step(k, total):
        sl = block(k)
        before = block(jnp.maximum(k - 1, 0))
        after = block(jnp.minimum(k + 1, nb - 1))
        edge_x = coords[0, :, sl] == 0
        edge_z = coords[1, :, sl] == 0
        second = (k >= hb).astype(jnp.int32)
        dst = block(k - second * hb)
        for a in range(8):
            x, y, z = alg[0, a, :, sl], alg[1, a, :, sl], alg[2, a, :, sl]
            near = pltpu.roll(jnp.where(lane == LANES - 1, alg[0, a, :, before], x), 1, 1)
            far = pltpu.roll(jnp.where(lane < extent - 1, alg[0, a, :, after], x), LANES - extent + 1, 1)
            bx = jnp.where(edge_x, far, near)
            by = jnp.where(
                k < yb,
                y_rim[a, :, block(jnp.minimum(k, yb - 1))],
                alg[1, a, :, block(jnp.maximum(k - yb, 0))],
            )
            prev = jnp.where(k == 0, z_below[a], alg[2, a, :, before])
            near = pltpu.roll(jnp.where(lane >= LANES - extent, prev, z), extent, 1)
            far = pltpu.roll(jnp.where(k == 0, alg[2, a, :, block(yb)], z_above[a]), extent, 1)
            bz = jnp.where(edge_z, far, near)
            b = (bx - x) + (by - y) + (bz - z)
            total = total + b * b
            mat[pl.ds(pl.multiple_of((a % 2) * HALF + second * (HALF // 2) + (a // 2) * 8, 8), 8), dst] = b
        return total

    theta[...] = lax.fori_loop(0, nb, step, jnp.zeros((8, LANES), f32))
    for k in range(hb):
        rows[k * LANES : (k + 1) * LANES, :] = mat[:, k * LANES : (k + 1) * LANES].T

    def dft(i, carry):
        parts = [rows[pl.ds(pl.multiple_of((2 * i + e) * extent, 8), extent), :] for e in range(2)]
        for e, v in enumerate(transform(table[...], parts, 1.0)):
            freq[pl.ds(pl.multiple_of((2 * i + e) * extent, 8), extent), :] = v
        return carry

    lax.fori_loop(0, qh // 2, dft, 0, unroll=4)
    count = extent // (out.shape[0] // nsplit)
    seg = lax.rem(lane_ids(qh), HALF) // SEG

    def pack(j, carry):
        vals = [freq[pl.ds(j * count + m, qh, stride=extent), :] for m in range(count)]
        for c in range(nsplit):
            full = []
            for h in range(2):
                acc = jnp.zeros((qh, LANES), f32)
                for m in range(count):
                    moved = pltpu.roll(vals[m], ((m - (2 * h + c)) * SEG) % LANES, 1)
                    acc = jnp.where(seg == m, moved, acc)
                full.append(acc[: qh if h == 0 else q - qh])
            out[j * nsplit + c] = pack_rows(jnp.concatenate(full, axis=0), count)
        return carry

    lax.fori_loop(0, out.shape[0] // nsplit, pack, 0, unroll=2)


def plane_kernel(extent, nsplit, planes, wave, table, out, one, two):
    n = extent
    total = n * n
    devices, kept = planes.shape[0], planes.shape[1]
    q = total // devices
    count = n * nsplit // devices
    scale = top_momentum / float(n) ** 3

    for s in range(devices):
        rows = unpack_rows(planes[s], q, count)
        if s == 0:
            one[0 : q - 1, :] = rows[1:]
            one[total - 1 : total, :] = rows[:1]
        else:
            one[s * q - 1 : (s + 1) * q - 1, :] = rows
    slot = jnp.minimum(lax.rem(lane_ids(n), HALF) // SEG, count - 1)
    kx = lax.div(lax.axis_index("space"), nsplit) * count + slot
    chosen = lax.broadcasted_iota(jnp.int32, (n, LANES), 0) == kx
    wave_lane = jnp.sum(jnp.where(chosen, wave[...], 0.0), axis=0, keepdims=True)

    def rows_at(i):
        return pl.ds(pl.multiple_of(i * n, 8), n)

    def along_z(i, carry):
        parts = [one[rows_at(2 * i + e), :] for e in range(2)]
        for e, v in enumerate(transform(table[...], parts, 1.0)):
            two[rows_at(2 * i + e), :] = v
        return carry

    lax.fori_loop(0, n // 2, along_z, 0, unroll=4)

    def along_y(i, carry):
        parts = [two[pl.ds(2 * i + e, n, stride=n), :] for e in range(2)]
        vals = transform(table[...], parts, 1.0)
        done = []
        for e, v in enumerate(vals):
            p2 = wave[...] + (wave_lane + wave[pl.ds(2 * i + e, 1), :])
            zero = p2 == 0.0
            done.append(v * jnp.where(zero, 0.0, scale / jnp.where(zero, 1.0, p2)))
        for e, v in enumerate(transform(table[...], done, -1.0)):
            one[rows_at(2 * i + e), :] = v
        return carry

    lax.fori_loop(0, n // 2, along_y, 0, unroll=4)

    def back_z(i, carry):
        parts = [one[pl.ds(2 * i + e, n, stride=n), :] for e in range(2)]
        for e, v in enumerate(transform(table[...], parts, -1.0)):
            two[rows_at(2 * i + e), :] = v
        return carry

    lax.fori_loop(0, n // 2, back_z, 0, unroll=4)
    for s in range(devices):
        if s == 0:
            rows = jnp.concatenate([two[total - 1 : total, :], two[0 : q - 1, :]], axis=0)
        else:
            rows = two[s * q - 1 : (s + 1) * q - 1, :]
        out[s] = pack_rows(rows, count)


def gather_kernel(extent, head, nsplit, planes, table, out, rows, freq):
    hb = head // LANES
    qh = head // extent
    nb = out.shape[-1] // LANES
    q = out.shape[-1] // extent
    rest = q - qh
    count = extent // (planes.shape[0] // nsplit)
    seg = lax.rem(lane_ids(rest), HALF) // SEG
    seg_tail = lax.rem(lane_ids(qh - rest), HALF) // SEG

    def unpack(j, carry):
        full = [unpack_rows(planes[j * nsplit + c], q, count) for c in range(nsplit)]
        for m in range(count):
            acc = jnp.zeros((rest, LANES), f32)
            tail = jnp.zeros((qh - rest, LANES), f32)
            for c in range(nsplit):
                for h in range(2):
                    s = 2 * h + c
                    shift = ((s - m) * SEG) % LANES
                    lo = h * qh
                    acc = jnp.where(seg == s, pltpu.roll(full[c][lo : lo + rest], shift, 1), acc)
                    if h == 0:
                        tail = jnp.where(
                            seg_tail == s, pltpu.roll(full[c][rest:qh], shift, 1), tail
                        )
            freq[pl.ds(j * count + m, qh, stride=extent), :] = jnp.concatenate([acc, tail], axis=0)
        return carry

    lax.fori_loop(0, planes.shape[0] // nsplit, unpack, 0, unroll=2)

    def dft(i, carry):
        parts = [freq[pl.ds(pl.multiple_of((2 * i + e) * extent, 8), extent), :] for e in range(2)]
        for e, v in enumerate(transform(table[...], parts, -1.0)):
            rows[pl.ds(pl.multiple_of((2 * i + e) * extent, 8), extent), :] = v
        return carry

    lax.fori_loop(0, qh // 2, dft, 0, unroll=4)
    for k in range(hb):
        turned = rows[k * LANES : (k + 1) * LANES, :].T
        for a in range(8):
            first = (a % 2) * HALF + (a // 2) * 8
            out[a, :, k * LANES : (k + 1) * LANES] = turned[first : first + 8]
            if hb + k < nb:
                second = first + HALF // 2
                out[a, :, (hb + k) * LANES : (hb + k + 1) * LANES] = turned[second : second + 8]


def link_kernel(extent, links, smooth, above, below, coords, out, deficit, rot):
    nb = smooth.shape[-1] // LANES
    yb = above.shape[-1] // LANES
    lane = lane_ids()

    def rotate(values, sl):
        g = rotation_of(values)
        for i in range(3):
            for j in range(3):
                for p in range(2):
                    rot[6 * i + 2 * j + p, :, sl] = g[i][j][p]

    def rotate_own(k, carry):
        rotate([smooth[a, :, block(k)] for a in range(8)], block(k))
        return carry

    def rotate_above(k, carry):
        rotate([above[a, :, block(k)] for a in range(8)], block(nb + k))
        return carry

    lax.fori_loop(0, nb, rotate_own, 0)
    lax.fori_loop(0, yb, rotate_above, 0)
    rotate([below[a] for a in range(8)], block(nb + yb))

    def step(k, total):
        sl = block(k)
        before = block(jnp.maximum(k - 1, 0))
        after = block(k + 1)
        wrap = block(jnp.where(k == yb, 0, nb + yb))
        edge_x = coords[0, :, sl] == extent - 1
        edge_z = coords[1, :, sl] == extent - 1

        def ahead_x(e):
            cur = rot[e, :, sl]
            near = pltpu.roll(jnp.where(lane == 0, rot[e, :, after], cur), LANES - 1, 1)
            far = pltpu.roll(jnp.where(lane >= LANES - extent + 1, rot[e, :, before], cur), extent - 1, 1)
            return jnp.where(edge_x, far, near)

        def ahead_y(e):
            return rot[e, :, block(k + yb)]

        def ahead_z(e):
            cur = rot[e, :, sl]
            near = pltpu.roll(jnp.where(lane < extent, rot[e, :, after], cur), LANES - extent, 1)
            far = pltpu.roll(rot[e, :, wrap], LANES - extent, 1)
            return jnp.where(edge_z, far, near)

        for d, ahead in enumerate((ahead_x, ahead_y, ahead_z)):
            u = load_link(links, d, sl)
            own = [[(rot[6 * i + 2 * j, :, sl], rot[6 * i + 2 * j + 1, :, sl]) for j in range(3)] for i in range(3)]
            left = [
                [dot_row(own[i], [u[k2][j] for k2 in range(3)], cmul) for j in range(3)]
                for i in range(3)
            ]
            for j in range(3):
                row = [(ahead(6 * j + 2 * c), ahead(6 * j + 2 * c + 1)) for c in range(3)]
                for i in range(2):
                    v = dot_row(left[i], row, mul_conj)
                    out[d, i, j, 0, :, sl] = v[0]
                    out[d, i, j, 1, :, sl] = v[1]
                    if i == j:
                        total = total + (1.0 - v[0])
                if j == 2:
                    total = total + (1.0 - dot_row(left[2], row, mul_conj)[0])
        return total

    deficit[...] = lax.fori_loop(0, nb, step, jnp.zeros((8, LANES), f32))


def greet(others):
    barrier = pltpu.get_barrier_semaphore()
    for other in others:
        pl.semaphore_signal(barrier, inc=1, device_id={"space": other}, device_id_type=MESH)
    return barrier


def exchange_kernel(n, blocks, out, send_sem, recv_sem):
    me = lax.axis_index("space")

    def partner(i):
        if n & (n - 1):
            return lax.rem(me + i, n)
        other = me
        for b in range(n.bit_length() - 1):
            if i >> b & 1:
                other = other + (1 << b) * (1 - 2 * lax.rem(lax.div(me, 1 << b), 2))
        return other

    barrier = greet([partner(i) for i in range(1, n)])
    out[me] = blocks[me]
    pl.semaphore_wait(barrier, n - 1)
    copies = []
    for i in reversed(range(1, n)):
        other = partner(i)
        copy = pltpu.make_async_remote_copy(
            src_ref=blocks.at[other],
            dst_ref=out.at[me],
            send_sem=send_sem.at[i],
            recv_sem=recv_sem.at[i],
            device_id={"space": other},
            device_id_type=MESH,
        )
        copy.start()
        copies.append(copy)
    for copy in copies:
        copy.wait()


def exchange(blocks, n, number):
    return call(
        functools.partial(exchange_kernel, n),
        jax.ShapeDtypeStruct(blocks.shape, f32),
        [pltpu.SemaphoreType.DMA((n,)), pltpu.SemaphoreType.DMA((n,))],
        blocks,
        params=pltpu.CompilerParams(collective_id=number, has_side_effects=True),
    )


def halo_kernel(n, moves, source, *refs):
    outs, (send_sem, recv_sem) = refs[:-2], refs[-2:]
    me = lax.axis_index("space")
    ahead, behind = lax.rem(me + 1, n), lax.rem(me + n - 1, n)
    barrier = greet([ahead, behind])
    pl.semaphore_wait(barrier, 2)
    odd = lax.rem(me, 2)
    copies = []
    for i, (direction, select) in enumerate(moves):
        copy = pltpu.make_async_remote_copy(
            src_ref=select(source, odd),
            dst_ref=outs[i],
            send_sem=send_sem.at[i],
            recv_sem=recv_sem.at[i],
            device_id={"space": ahead if direction > 0 else behind},
            device_id_type=MESH,
        )
        copy.start()
        copies.append(copy)
    for copy in copies:
        copy.wait()


def halos(source, n, moves, shapes, number):
    count = len(moves)
    return call(
        functools.partial(halo_kernel, n, moves),
        shapes,
        [pltpu.SemaphoreType.DMA((count,)), pltpu.SemaphoreType.DMA((count,))],
        source,
        params=pltpu.CompilerParams(collective_id=number, has_side_effects=True),
    )


def sum_kernel(n, scales, theta, deficit, out_theta, out_deficit, mine, held, send_sem, recv_sem):
    me = lax.axis_index("space")
    barrier = greet([lax.rem(me + i, n) for i in range(1, n)])
    slices = deficit.shape[0]
    lane = lane_ids(slices)
    t = jnp.sum(jnp.sum(theta[...], axis=1, keepdims=True), axis=0, keepdims=True)
    d = jnp.sum(deficit[...], axis=1, keepdims=True)
    own = lax.broadcasted_iota(jnp.int32, (slices, LANES), 0)
    mine[...] = jnp.where(lane == own, d, jnp.where(lane == slices, jnp.where(own == 0, t, 0.0), 0.0))
    pl.semaphore_wait(barrier, n - 1)
    copies = []
    for i in range(1, n):
        copy = pltpu.make_async_remote_copy(
            src_ref=mine,
            dst_ref=held.at[i],
            send_sem=send_sem.at[i],
            recv_sem=recv_sem.at[i],
            device_id={"space": lax.rem(me + i, n)},
            device_id_type=MESH,
        )
        copy.start()
        copies.append(copy)
    for copy in copies:
        copy.wait()
    total = mine[...]
    for i in range(1, n):
        total = total + held[i]
    row = jnp.sum(total, axis=0, keepdims=True)
    out_deficit[...] = row[:, :slices] * scales[1]
    out_theta[...] = row[:, slices : slices + 1] * scales[0]


def call(kernel, out_shape, scratch, *args, params=PARAMS):
    return pl.pallas_call(
        kernel,
        out_shape=out_shape,
        in_specs=[VM] * len(args),
        out_specs=jax.tree.map(lambda _: VM, out_shape),
        scratch_shapes=scratch,
        compiler_params=params,
    )(*args)


def dft_table(n):
    k = np.arange(n)
    angle = 2.0 * np.pi / n * ((k[:, None] * k[None, :]) % n)
    full = np.concatenate([np.cos(angle), np.sin(angle)], axis=0).astype(np.float32)
    hi = full.astype(jnp.bfloat16)
    lo = (full - hi.astype(np.float32)).astype(jnp.bfloat16)
    return np.concatenate([hi, hi, lo], axis=1)


def body(links):
    n = EXTENT
    slices, local = links.shape[0], links.shape[-1]
    devices = lax.axis_size("space")
    plane = n * n
    q = local // n
    me = lax.axis_index("space")
    shape = lambda *s: jax.ShapeDtypeStruct(s, f32)


    table = jnp.asarray(dft_table(n))
    site = jnp.arange(local, dtype=jnp.int32)
    coords = jnp.stack([site % n, (me * q + site // n - 1) % n])
    coords = jnp.broadcast_to(coords[:, None, :], (2, slices, local))
    across = jnp.transpose(links, (1, 2, 3, 4, 0, 5))
    alg = call(algebra_kernel, shape(3, 8, slices, local), [], across)
    mid = (n // 2) * n
    side = lambda start: pl.ds(pl.multiple_of(start, LANES), LANES)
    y_rim, z_below, z_above = halos(
        alg,
        devices,
        [
            (1, lambda r, odd: r.at[1, :, :, local - plane :]),
            (1, lambda r, odd: r.at[2, :, :, local - LANES :]),
            (-1, lambda r, odd: r.at[2, :, :, side(odd * mid)]),
        ],
        (shape(8, slices, plane), shape(8, slices, LANES), shape(8, slices, LANES)),
        2,
    )
    head = -(-(local // 2) // (8 * n)) * 8 * n
    qh = head // n
    nsplit = 2
    kept = packed_rows(q, n * nsplit // devices)
    spread, theta = call(
        functools.partial(spread_kernel, n, head, nsplit, q),
        (shape(devices, kept, LANES), shape(slices, LANES)),
        [pltpu.VMEM((LANES, head), f32), pltpu.VMEM((head, LANES), f32), pltpu.VMEM((head, LANES), f32)],
        alg, y_rim, z_below, z_above, coords, table,
    )
    planes = exchange(spread, devices, 3)
    wave_np = (4.0 * np.sin(np.pi * np.arange(n) / n) ** 2).astype(np.float32)
    wave = jnp.asarray(np.ascontiguousarray(np.broadcast_to(wave_np[:, None], (n, LANES))))
    smoothed = call(
        functools.partial(plane_kernel, n, nsplit),
        shape(devices, kept, LANES),
        [pltpu.VMEM((plane, LANES), f32), pltpu.VMEM((plane, LANES), f32)],
        planes, wave, table,
    )
    back = exchange(smoothed, devices, 4)
    smooth = call(
        functools.partial(gather_kernel, n, head, nsplit),
        shape(8, slices, local),
        [pltpu.VMEM((head, LANES), f32), pltpu.VMEM((head, LANES), f32)],
        back, table,
    )
    above, below = halos(
        smooth,
        devices,
        [
            (-1, lambda r, odd: r.at[:, :, :plane]),
            (1, lambda r, odd: r.at[:, :, side(plane - odd * (plane - mid))]),
        ],
        (shape(8, slices, plane), shape(8, slices, LANES)),
        5,
    )
    turned, deficit = call(
        functools.partial(link_kernel, n),
        (shape(3, 2, 3, 2, slices, local), shape(slices, LANES)),
        [pltpu.VMEM((18, slices, local + plane + LANES), f32)],
        across, smooth, above, below, coords,
    )
    new_links = jnp.transpose(turned, (4, 0, 1, 2, 3, 5))
    times = lax.axis_size("tm")
    scales = (1.0 / (slices * times * n**3), 1.0 / n**3)
    total, shares = call(
        functools.partial(sum_kernel, devices, scales),
        (shape(1, 1), shape(1, slices)),
        [
            pltpu.VMEM((slices, LANES), f32),
            pltpu.VMEM((devices, slices, LANES), f32),
            pltpu.SemaphoreType.DMA((devices,)),
            pltpu.SemaphoreType.DMA((devices,)),
        ],
        theta, deficit,
        params=pltpu.CompilerParams(collective_id=1, has_side_effects=True),
    )
    total = total.reshape(())
    if times > 1:
        total = lax.psum(total, "tm")
    return (new_links, total, shares.reshape(slices))


def solution(mesh):
    placed = (P("tm", None, None, None, None, "space"),)
    return jax.shard_map(
        body,
        mesh=mesh,
        in_specs=placed,
        out_specs=(P("tm", None, None, None, None, "space"), P(), P("tm")),
        check_vma=False,
    )
```

profile of v0, /device:TPU:0, one launch (start us, length us, event | category | flops | bytes accessed | tf_op | source)
XLA Modules:
  0.0 148.5 jit_solution(11400114935894707119)
XLA Ops:
  0.6 0.1 and_select_fusion
  0.8 0.7 broadcast_in_dim.2.coords
  1.5 4.3 %copy.9 = f32[8,3,2,3,2,3456]{5,0,4,3,2,1:T(8,128)} copy(f32[8,3,2,3,2,3456]{5,4,3,2,1,0:T(2,128)} %param.3) | data formatting | bytes 7962624 | tf_op args[0]
  5.8 4.4 %shard_map.58.source.alg = f32[3,8,8,3456]{3,2,1,0:T(8,128)} custom-call(f32[3,2,3,2,8,3456]{5,4,3,2,1,0:T(8,128)} %bitcast.6), custom_call_target="tpu_custom_call" | custom-call | tf_op jit(solution)/shard_map/pallas_call | solution.py:553
  10.3 17.6 %shard_map.59 = (f32[8,8,2304]{2,1,0:T(8,128)}, f32[8,8,128]{2,1,0:T(8,128)}, f32[8,8,128]{2,1,0:T(8,128)}) custom-call(f32[3,8,8,3456]{3,2,1,0:T(8,128)} %shard_map.58.source.alg), custom_call_target="tpu_custom_call" | custom-call | tf_op jit(solution)/shard_map/pallas_call | solution.py:553
  27.9 9.6 %shard_map.60 = (f32[32,56,128]{2,1,0:T(8,128)}, f32[8,128]{1,0:T(8,128)}) custom-call(f32[3,8,8,3456]{3,2,1,0:T(8,128)} %shard_map.58.source.alg, f32[8,8,2304]{2,1,0:T(8,128)} %get-tuple-element.14.y_rim, f32[8,8,128]{2,1,0:T(8,128)} %get-tuple-element.15.z_below, f32[8,8,128]{2,1,0:T(8,128)} %get-tuple-element.16.z_above, ...), custom_call_target="tpu_custom_call" | custom-call | tf_op jit(solution)/shard_map/pallas_call | solution.py:553
  37.5 26.6 %shard_map.61.planes = f32[32,56,128]{2,1,0:T(8,128)} custom-call(f32[32,56,128]{2,1,0:T(8,128)} %get-tuple-element.17.blocks), custom_call_target="tpu_custom_call" | custom-call | tf_op jit(solution)/shard_map/pallas_call | solution.py:553
  64.1 9.6 %shard_map.62.blocks = f32[32,56,128]{2,1,0:T(8,128)} custom-call(f32[32,56,128]{2,1,0:T(8,128)} %shard_map.61.planes, f32[48,128]{1,0:T(8,128)} %constant.36.clone.wave, bf16[96,144]{1,0:T(8,128)(2,1)} %constant.35.clone.table), custom_call_target="tpu_custom_call" | custom-call | tf_op jit(solution)/shard_map/pallas_call | solution.py:553
  73.7 27.9 %shard_map.63.planes = f32[32,56,128]{2,1,0:T(8,128)} custom-call(f32[32,56,128]{2,1,0:T(8,128)} %shard_map.62.blocks), custom_call_target="tpu_custom_call" | custom-call | tf_op jit(solution)/shard_map/pallas_call | solution.py:553
  101.6 5.5 %shard_map.64.source.smooth = f32[8,8,3456]{2,1,0:T(8,128)} custom-call(f32[32,56,128]{2,1,0:T(8,128)} %shard_map.63.planes, bf16[96,144]{1,0:T(8,128)(2,1)} %constant.35.clone.table), custom_call_target="tpu_custom_call" | custom-call | tf_op jit(solution)/shard_map/pallas_call | solution.py:553
  107.1 10.8 %shard_map.65 = (f32[8,8,2304]{2,1,0:T(8,128)}, f32[8,8,128]{2,1,0:T(8,128)}) custom-call(f32[8,8,3456]{2,1,0:T(8,128)} %shard_map.64.source.smooth), custom_call_target="tpu_custom_call" | custom-call | tf_op jit(solution)/shard_map/pallas_call | solution.py:553
  117.9 12.1 %shard_map.66 = (f32[3,2,3,2,8,3456]{5,4,3,2,1,0:T(8,128)}, f32[8,128]{1,0:T(8,128)}) custom-call(f32[3,2,3,2,8,3456]{5,4,3,2,1,0:T(8,128)} %bitcast.7, f32[8,8,3456]{2,1,0:T(8,128)} %shard_map.64.source.smooth, f32[8,8,2304]{2,1,0:T(8,128)} %get-tuple-element.18.above, f32[8,8,128]{2,1,0:T(8,128)} %get-tuple-element.19.below, ...), custom_call_target="tpu_custom_call" | custom-call | tf_op jit(solution)/shard_map/pallas_call | solution.py:553
  129.9 10.2 %shard_map.67 = (f32[1,1]{1,0:T(1,128)}, f32[1,8]{1,0:T(1,128)}) custom-call(f32[8,128]{1,0:T(8,128)} %get-tuple-element.21.theta, f32[8,128]{1,0:T(8,128)} %get-tuple-element.22.deficit), custom_call_target="tpu_custom_call" | custom-call | tf_op jit(solution)/shard_map/pallas_call | solution.py:553
  140.2 0.0 copy-start
  140.2 6.1 %copy.7 = f32[8,3,2,3,2,3456]{5,4,3,2,1,0:T(2,128)} copy(f32[8,3,2,3,2,3456]{5,0,4,3,2,1:T(8,128)} %bitcast.8) | data formatting | bytes 7962624
  146.9 0.0 copy-done
  146.9 0.5 copy.13
  (1 shorter events, 0.0 us)
Async XLA Ops:
  140.2 6.7 %copy-start = (f32[1,8]{1,0:T(1,128)S(1)}, f32[1,8]{1,0:T(1,128)}, u32[]{:S(2)}) copy-start(f32[1,8]{1,0:T(1,128)} %get-tuple-element.24) | copy-start | bytes 100
where the time goes:
time: 149 us
  Pallas kernels  134 us (90%)
  local copies, waits for them, and re-layouts  11.7 us (8%)
  between operations  2.39 us (2%)
    pallas_call x10, Pallas kernels, call(): pl.pallas_call(kernel, out_shape=out_shape, in_specs=[VM] * len(args), ou...  134 us
    unnamed x5, local copies, waits for them, and re-layouts  11 us

commit v1 on v0

--- a/solution.py
+++ b/solution.py
@@ -11,8 +11,8 @@
 
 EXTENT = 48
 LANES = 128
-HALF = 64
-SEG = 16
+UNITS = 3
+PIECES = 6
 
 root_three = math.sqrt(3.0)
 step_size = 0.08
@@ -149,57 +149,36 @@
     return jnp.concatenate([hi, lo, hi], axis=0)
 
 
-def transform(table, parts, sign):
-    n = parts[0].shape[0]
+def transform(table, parts):
     both = jnp.dot(table, split3(jnp.concatenate(parts, axis=1)), preferred_element_type=f32)
-    outs = []
-    for i in range(len(parts)):
-        mine = both[:, i * LANES : (i + 1) * LANES]
-        swapped = pltpu.roll(mine[n:], HALF, 1)
-        outs.append(mine[:n] + jnp.where(lane_ids(n) < HALF, sign, -sign) * swapped)
-    return outs
-
-
-def packed_rows(q, count):
-    free = HALF // SEG - count
-    moved = -(-q * free // (count + free)) // 8 * 8
-    return q - moved if free == 1 else q
-
-
-def pack_rows(full, count):
-    q = full.shape[0]
-    kept = packed_rows(q, count)
-    step = q - kept
-    if step == 0:
-        return full
-    seg = lax.rem(lane_ids(step), HALF) // SEG
-    pieces = []
-    for m in range(count):
-        moved = pltpu.roll(full[kept:], (count - m) * SEG, 1)
-        pieces.append(jnp.where(seg == count, moved, full[m * step : (m + 1) * step]))
-    return jnp.concatenate(pieces + [full[count * step : kept]], axis=0)
-
-
-def unpack_rows(block_in, q, count):
-    kept = block_in.shape[0]
-    step = q - kept
-    if step == 0:
-        return block_in
-    seg = lax.rem(lane_ids(step), HALF) // SEG
-    tail = jnp.zeros((step, LANES), f32)
-    for m in range(count):
-        moved = pltpu.roll(block_in[m * step : (m + 1) * step], LANES - (count - m) * SEG, 1)
-        tail = jnp.where(seg == m, moved, tail)
-    return jnp.concatenate([block_in, tail], axis=0)
-
-
-def spread_kernel(extent, head, nsplit, q, alg, y_rim, z_below, z_above, coords, table, out, theta, mat, rows, freq):
+    return [both[:, i * LANES : (i + 1) * LANES] for i in range(len(parts))]
+
+
+def swap(v):
+    return pltpu.roll(v, 4, 0)
+
+
+def flip(place, i, group):
+    other = place
+    for b in range(group.bit_length() - 1):
+        if i >> b & 1:
+            other = other + (1 << b) * (1 - 2 * lax.rem(lax.div(place, 1 << b), 2))
+    return other
+
+
+def spread_kernel(
+    extent, group, alg, y_rim, z_below, z_above, coords, out, theta, mine, send_sem, recv_sem, edge_send, edge_recv
+):
     nb = alg.shape[-1] // LANES
     yb = y_rim.shape[-1] // LANES
-    qh = head // extent
-    hb = head // LANES
+    half = alg.shape[2] // 2
+    third = nb // UNITS
     lane = lane_ids()
-    mat[...] = jnp.zeros_like(mat)
+    me = lax.axis_index("space")
+    place = lax.rem(me, group)
+    base = me - place
+    beyond = group - base
+    barrier = greet([base + flip(place, i, group) for i in range(1, group)] + [beyond + i for i in range(group)])
 
     def step(k, total):
         sl = block(k)
@@ -207,8 +186,6 @@
         after = block(jnp.minimum(k + 1, nb - 1))
         edge_x = coords[0, :, sl] == 0
         edge_z = coords[1, :, sl] == 0
-        second = (k >= hb).astype(jnp.int32)
-        dst = block(k - second * hb)
         for a in range(8):
             x, y, z = alg[0, a, :, sl], alg[1, a, :, sl], alg[2, a, :, sl]
             near = pltpu.roll(jnp.where(lane == LANES - 1, alg[0, a, :, before], x), 1, 1)
@@ -225,144 +202,293 @@
             bz = jnp.where(edge_z, far, near)
             b = (bx - x) + (by - y) + (bz - z)
             total = total + b * b
-            mat[pl.ds(pl.multiple_of((a % 2) * HALF + second * (HALF // 2) + (a // 2) * 8, 8), 8), dst] = b
+            mine[2 * a, k] = b[:half]
+            mine[2 * a + 1, k] = b[half:]
         return total
 
-    theta[...] = lax.fori_loop(0, nb, step, jnp.zeros((8, LANES), f32))
-    for k in range(hb):
-        rows[k * LANES : (k + 1) * LANES, :] = mat[:, k * LANES : (k + 1) * LANES].T
-
-    def dft(i, carry):
-        parts = [rows[pl.ds(pl.multiple_of((2 * i + e) * extent, 8), extent), :] for e in range(2)]
-        for e, v in enumerate(transform(table[...], parts, 1.0)):
-            freq[pl.ds(pl.multiple_of((2 * i + e) * extent, 8), extent), :] = v
-        return carry
-
-    lax.fori_loop(0, qh // 2, dft, 0, unroll=4)
-    count = extent // (out.shape[0] // nsplit)
-    seg = lax.rem(lane_ids(qh), HALF) // SEG
-
-    def pack(j, carry):
-        vals = [freq[pl.ds(j * count + m, qh, stride=extent), :] for m in range(count)]
-        for c in range(nsplit):
-            full = []
-            for h in range(2):
-                acc = jnp.zeros((qh, LANES), f32)
-                for m in range(count):
-                    moved = pltpu.roll(vals[m], ((m - (2 * h + c)) * SEG) % LANES, 1)
-                    acc = jnp.where(seg == m, moved, acc)
-                full.append(acc[: qh if h == 0 else q - qh])
-            out[j * nsplit + c] = pack_rows(jnp.concatenate(full, axis=0), count)
-        return carry
-
-    lax.fori_loop(0, out.shape[0] // nsplit, pack, 0, unroll=2)
-
-
-def plane_kernel(extent, nsplit, planes, wave, table, out, one, two):
+    def edge_copy(i):
+        return pltpu.make_async_remote_copy(
+            src_ref=mine.at[i, pl.ds(0, 1)],
+            dst_ref=out.at[pl.ds(group * nb, 1)],
+            send_sem=edge_send.at[i],
+            recv_sem=edge_recv.at[0],
+            device_id={"space": beyond + i},
+            device_id_type=MESH,
+        )
+
+    total = jnp.zeros((8, LANES), f32)
+    copies = []
+    for c in range(UNITS):
+        total = lax.fori_loop(c * third, (c + 1) * third, step, total)
+        if c == 0:
+            pl.semaphore_wait(barrier, 2 * group - 1)
+
+            @pl.when(place == 0)
+            def _():
+                for i in range(group):
+                    edge_copy(i).start()
+
+        for i in reversed(range(1, group)):
+            other = flip(place, i, group)
+            copy = pltpu.make_async_remote_copy(
+                src_ref=mine.at[other, pl.ds(c * third, third)],
+                dst_ref=out.at[pl.ds(place * nb + c * third, third)],
+                send_sem=send_sem.at[c, i],
+                recv_sem=recv_sem.at[c, i],
+                device_id={"space": base + other},
+                device_id_type=MESH,
+            )
+            copy.start()
+            copies.append(copy)
+    theta[...] = total
+
+    def keep(k, carry):
+        out[place * nb + k] = mine[place, k]
+        return carry
+
+    lax.fori_loop(0, nb, keep, 0)
+    for copy in copies:
+        copy.wait()
+    edge_copy(0).wait_recv()
+
+    @pl.when(place == 0)
+    def _():
+        for i in range(group):
+            edge_copy(i).wait_send()
+
+
+def solve_kernel(
+    extent, group, fields, decay, weight, close, x_table, z_table, z_back, own_zero, far_zero,
+    smooth, one, two, modes, ends, far, mode, far_mode, outgo, held, edge_held,
+    end_send, end_recv, send_sem, recv_sem, edge_send, edge_recv,
+):
     n = extent
-    total = n * n
-    devices, kept = planes.shape[0], planes.shape[1]
-    q = total // devices
-    count = n * nsplit // devices
-    scale = top_momentum / float(n) ** 3
-
-    for s in range(devices):
-        rows = unpack_rows(planes[s], q, count)
-        if s == 0:
-            one[0 : q - 1, :] = rows[1:]
-            one[total - 1 : total, :] = rows[:1]
-        else:
-            one[s * q - 1 : (s + 1) * q - 1, :] = rows
-    slot = jnp.minimum(lax.rem(lane_ids(n), HALF) // SEG, count - 1)
-    kx = lax.div(lax.axis_index("space"), nsplit) * count + slot
-    chosen = lax.broadcasted_iota(jnp.int32, (n, LANES), 0) == kx
-    wave_lane = jnp.sum(jnp.where(chosen, wave[...], 0.0), axis=0, keepdims=True)
+    nb = smooth.shape[-1] // LANES
+    planes = group * nb * LANES // (n * n)
+    columns = n * n // LANES
+    pairs = planes // 2
+    lanes = planes * 4
+    per = columns // PIECES
+    unit = nb // UNITS
+    me = lax.axis_index("space")
+    place = lax.rem(me, group)
+    base = me - place
+    beyond = group - base
+    upper = lax.broadcasted_iota(jnp.int32, (8, LANES), 0) >= 4
+    barrier = greet([base + flip(place, i, group) for i in range(1, group)] + [beyond + i for i in range(group)])
 
     def rows_at(i):
         return pl.ds(pl.multiple_of(i * n, 8), n)
 
+    def turn_in(c, extra):
+        tiles = [fields[y * columns + c] for y in range(planes)] + extra
+        rest = LANES - 4 * len(tiles)
+        full = jnp.concatenate(tiles + [jnp.zeros((rest, LANES), f32)], axis=0)
+        one[block(c), :] = full.T
+
+    turn_in(0, [fields[planes * columns]])
+
+    def turn_rest(c, carry):
+        turn_in(c, [])
+        return carry
+
+    lax.fori_loop(1, columns, turn_rest, 0)
+    one[0:n, :] = pltpu.roll(one[0:n, :], LANES - 4, 1)
+
+    def along_x(i, carry):
+        parts = [one[rows_at(2 * i + e), :] for e in range(2)]
+        for e, v in enumerate(transform(x_table[...], parts)):
+            two[rows_at(2 * i + e), :] = v
+        return carry
+
+    lax.fori_loop(0, n // 2, along_x, 0, unroll=4)
+
     def along_z(i, carry):
+        parts = [two[pl.ds(2 * i + e, n, stride=n), :] for e in range(2)]
+        for e, v in enumerate(transform(z_table[...], parts)):
+            one[rows_at(2 * i + e), :] = v
+        return carry
+
+    def end_copy(p):
+        cols = pl.ds(p * per * LANES, per * LANES)
+        return pltpu.make_async_remote_copy(
+            src_ref=ends.at[:, cols],
+            dst_ref=far.at[:, cols],
+            send_sem=end_send.at[p],
+            recv_sem=end_recv.at[p],
+            device_id={"space": beyond + place},
+            device_id_type=MESH,
+        )
+
+    mode_copy = pltpu.make_async_remote_copy(
+        src_ref=mode,
+        dst_ref=far_mode,
+        send_sem=end_send.at[PIECES],
+        recv_sem=end_recv.at[PIECES],
+        device_id={"space": beyond + place},
+        device_id_type=MESH,
+    )
+
+    def reduce_ends(c, carry):
+        sl = block(c)
+        modes[:, sl] = one[sl, :].T[:lanes]
+        mu = decay[:, sl]
+        mu2 = mu * mu
+        low = jnp.where(upper, 1.0, mu)
+        high = jnp.where(upper, mu, 1.0)
+        fwd = modes[0:8, sl]
+        bwd = modes[lanes - 8 : lanes, sl]
+        for i in range(1, pairs):
+            fwd = fwd * mu2 + modes[8 * i : 8 * i + 8, sl]
+            bwd = bwd * mu2 + modes[lanes - 8 - 8 * i : lanes - 8 * i, sl]
+        ends[:, sl] = jnp.where(upper, high * bwd + low * swap(bwd), low * fwd + high * swap(fwd))
+        return carry
+
+    step_z = n // 2 // PIECES
+    for p in range(PIECES):
+        lax.fori_loop(p * step_z, (p + 1) * step_z, along_z, 0, unroll=4)
+        if p == 0:
+            mode[...] = one[0:8, :]
+        lax.fori_loop(p * per, (p + 1) * per, reduce_ends, 0)
+        if p == 0:
+            pl.semaphore_wait(barrier, 2 * group - 1)
+            mode_copy.start()
+        end_copy(p).start()
+
+    def sweep(c, carry):
+        sl = block(c)
+        mu = decay[:, sl]
+        mu2 = mu * mu
+        low = jnp.where(upper, 1.0, mu)
+        high = jnp.where(upper, mu, 1.0)
+        total = close[0, :, sl] * far[:, sl] + close[1, :, sl] * ends[:, sl]
+        turned = swap(total)
+        e = jnp.where(upper, turned, total)
+        f = jnp.where(upper, total, turned) * mu
+        w = weight[:, sl]
+        up = mu * high
+        down = jnp.where(upper, 0.0, mu)
+        rising = []
+        for i in range(pairs):
+            v = modes[8 * i : 8 * i + 8, sl]
+            s = low * v + high * swap(v)
+            rising.append(jnp.where(upper, s, v) + up * e)
+            e = mu2 * e + s
+        done = [None] * pairs
+        for i in reversed(range(pairs)):
+            v = modes[8 * i : 8 * i + 8, sl]
+            t = swap(v)
+            done[i] = w * (rising[i] + low * f + down * t)
+            f = mu2 * f + mu * (high * v + low * t)
+        full = jnp.concatenate(done + [jnp.zeros((LANES - lanes, LANES), f32)], axis=0)
+        one[sl, :] = full.T
+        return carry
+
+    def back_z(i, carry):
         parts = [one[rows_at(2 * i + e), :] for e in range(2)]
-        for e, v in enumerate(transform(table[...], parts, 1.0)):
-            two[rows_at(2 * i + e), :] = v
-        return carry
-
-    lax.fori_loop(0, n // 2, along_z, 0, unroll=4)
-
-    def along_y(i, carry):
-        parts = [two[pl.ds(2 * i + e, n, stride=n), :] for e in range(2)]
-        vals = transform(table[...], parts, 1.0)
-        done = []
-        for e, v in enumerate(vals):
-            p2 = wave[...] + (wave_lane + wave[pl.ds(2 * i + e, 1), :])
-            zero = p2 == 0.0
-            done.append(v * jnp.where(zero, 0.0, scale / jnp.where(zero, 1.0, p2)))
-        for e, v in enumerate(transform(table[...], done, -1.0)):
+        for e, v in enumerate(transform(z_back[...], parts)):
+            two[pl.ds(2 * i + e, n, stride=n), :] = v
+        return carry
+
+    for p in range(PIECES):
+        end_copy(p).wait_recv()
+        if p == 0:
+            mode_copy.wait_recv()
+        lax.fori_loop(p * per, (p + 1) * per, sweep, 0)
+        if p == 0:
+            exact = functools.partial(jnp.dot, preferred_element_type=f32, precision=lax.Precision.HIGHEST)
+            flat = exact(mode[...], own_zero[...]) + exact(far_mode[...], far_zero[...])
+            first = lax.broadcasted_iota(jnp.int32, (8, LANES), 0) == 0
+            one[0:8, :] = jnp.where(first, flat, one[0:8, :])
+        lax.fori_loop(p * step_z, (p + 1) * step_z, back_z, 0, unroll=4)
+
+    def back_x(i, carry):
+        parts = [two[rows_at(2 * i + e), :] for e in range(2)]
+        for e, v in enumerate(transform(x_table[...], parts)):
             one[rows_at(2 * i + e), :] = v
         return carry
 
-    lax.fori_loop(0, n // 2, along_y, 0, unroll=4)
-
-    def back_z(i, carry):
-        parts = [one[pl.ds(2 * i + e, n, stride=n), :] for e in range(2)]
-        for e, v in enumerate(transform(table[...], parts, -1.0)):
-            two[rows_at(2 * i + e), :] = v
-        return carry
-
-    lax.fori_loop(0, n // 2, back_z, 0, unroll=4)
-    for s in range(devices):
-        if s == 0:
-            rows = jnp.concatenate([two[total - 1 : total, :], two[0 : q - 1, :]], axis=0)
-        else:
-            rows = two[s * q - 1 : (s + 1) * q - 1, :]
-        out[s] = pack_rows(rows, count)
-
-
-def gather_kernel(extent, head, nsplit, planes, table, out, rows, freq):
-    hb = head // LANES
-    qh = head // extent
-    nb = out.shape[-1] // LANES
-    q = out.shape[-1] // extent
-    rest = q - qh
-    count = extent // (planes.shape[0] // nsplit)
-    seg = lax.rem(lane_ids(rest), HALF) // SEG
-    seg_tail = lax.rem(lane_ids(qh - rest), HALF) // SEG
-
-    def unpack(j, carry):
-        full = [unpack_rows(planes[j * nsplit + c], q, count) for c in range(nsplit)]
-        for m in range(count):
-            acc = jnp.zeros((rest, LANES), f32)
-            tail = jnp.zeros((qh - rest, LANES), f32)
-            for c in range(nsplit):
-                for h in range(2):
-                    s = 2 * h + c
-                    shift = ((s - m) * SEG) % LANES
-                    lo = h * qh
-                    acc = jnp.where(seg == s, pltpu.roll(full[c][lo : lo + rest], shift, 1), acc)
-                    if h == 0:
-                        tail = jnp.where(
-                            seg_tail == s, pltpu.roll(full[c][rest:qh], shift, 1), tail
-                        )
-            freq[pl.ds(j * count + m, qh, stride=extent), :] = jnp.concatenate([acc, tail], axis=0)
-        return carry
-
-    lax.fori_loop(0, planes.shape[0] // nsplit, unpack, 0, unroll=2)
-
-    def dft(i, carry):
-        parts = [freq[pl.ds(pl.multiple_of((2 * i + e) * extent, 8), extent), :] for e in range(2)]
-        for e, v in enumerate(transform(table[...], parts, -1.0)):
-            rows[pl.ds(pl.multiple_of((2 * i + e) * extent, 8), extent), :] = v
-        return carry
-
-    lax.fori_loop(0, qh // 2, dft, 0, unroll=4)
-    for k in range(hb):
-        turned = rows[k * LANES : (k + 1) * LANES, :].T
+    lax.fori_loop(0, n // 2, back_x, 0, unroll=4)
+    one[0:n, :] = pltpu.roll(one[0:n, :], 4, 1)
+
+    def turn_out(c):
+        full = one[block(c), :].T
+        for y in range(planes):
+            outgo[y * columns + c] = full[4 * y : 4 * y + 4]
+        return full
+
+    def turn_out_rest(c, carry):
+        turn_out(c)
+        return carry
+
+    def unit_copy(i, v):
+        other = flip(place, i, group)
+        return pltpu.make_async_remote_copy(
+            src_ref=outgo.at[pl.ds(other * nb + v * unit, unit)],
+            dst_ref=held.at[place, pl.ds(v * unit, unit)],
+            send_sem=send_sem.at[v, i],
+            recv_sem=recv_sem.at[v, i],
+            device_id={"space": base + other},
+            device_id_type=MESH,
+        )
+
+    edge_copy = pltpu.make_async_remote_copy(
+        src_ref=outgo.at[pl.ds(planes * columns, 1)],
+        dst_ref=edge_held.at[place],
+        send_sem=edge_send.at[0],
+        recv_sem=edge_recv.at[place],
+        device_id={"space": beyond},
+        device_id_type=MESH,
+    )
+
+    full = turn_out(0)
+    outgo[planes * columns] = full[lanes : lanes + 4]
+    for side in range(2):
+        lax.fori_loop(max(1, side * unit), (side + 1) * unit, turn_out_rest, 0)
+        if side == 0:
+            edge_copy.start()
+        for i in reversed(range(1, group)):
+            odd = lax.rem(place + i + side, 2)
+            unit_copy(i, odd).start()
+
+            @pl.when(odd == 0)
+            def _():
+                unit_copy(i, 2).start()
+
+    def keep(k, carry):
+        held[place, k] = outgo[place * nb + k]
+        return carry
+
+    lax.fori_loop(0, nb, keep, 0)
+    for p in range(PIECES):
+        end_copy(p).wait_send()
+    mode_copy.wait_send()
+    for i in reversed(range(1, group)):
+        for v in range(UNITS):
+            unit_copy(i, v).wait()
+
+    def gather(k, carry):
         for a in range(8):
-            first = (a % 2) * HALF + (a // 2) * 8
-            out[a, :, k * LANES : (k + 1) * LANES] = turned[first : first + 8]
-            if hb + k < nb:
-                second = first + HALF // 2
-                out[a, :, (hb + k) * LANES : (hb + k + 1) * LANES] = turned[second : second + 8]
+            smooth[a, :, block(k)] = jnp.concatenate([held[2 * a, k], held[2 * a + 1, k]], axis=0)
+        return carry
+
+    lax.fori_loop(0, nb, gather, 0)
+    edge_copy.wait_send()
+
+    @pl.when(place == 0)
+    def _():
+        for i in range(group):
+            pltpu.make_async_remote_copy(
+                src_ref=outgo.at[pl.ds(planes * columns, 1)],
+                dst_ref=edge_held.at[i],
+                send_sem=edge_send.at[0],
+                recv_sem=edge_recv.at[i],
+                device_id={"space": beyond},
+                device_id_type=MESH,
+            ).wait_recv()
+        for a in range(8):
+            row = jnp.concatenate([edge_held[2 * a, 0], edge_held[2 * a + 1, 0]], axis=0)
+            smooth[a, :, 0:LANES] = jnp.where(lane_ids() < n, row, smooth[a, :, 0:LANES])
 
 
 def link_kernel(extent, links, smooth, above, below, coords, out, deficit, rot):
@@ -439,48 +565,6 @@
     for other in others:
         pl.semaphore_signal(barrier, inc=1, device_id={"space": other}, device_id_type=MESH)
     return barrier
-
-
-def exchange_kernel(n, blocks, out, send_sem, recv_sem):
-    me = lax.axis_index("space")
-
-    def partner(i):
-        if n & (n - 1):
-            return lax.rem(me + i, n)
-        other = me
-        for b in range(n.bit_length() - 1):
-            if i >> b & 1:
-                other = other + (1 << b) * (1 - 2 * lax.rem(lax.div(me, 1 << b), 2))
-        return other
-
-    barrier = greet([partner(i) for i in range(1, n)])
-    out[me] = blocks[me]
-    pl.semaphore_wait(barrier, n - 1)
-    copies = []
-    for i in reversed(range(1, n)):
-        other = partner(i)
-        copy = pltpu.make_async_remote_copy(
-            src_ref=blocks.at[other],
-            dst_ref=out.at[me],
-            send_sem=send_sem.at[i],
-            recv_sem=recv_sem.at[i],
-            device_id={"space": other},
-            device_id_type=MESH,
-        )
-        copy.start()
-        copies.append(copy)
-    for copy in copies:
-        copy.wait()
-
-
-def exchange(blocks, n, number):
-    return call(
-        functools.partial(exchange_kernel, n),
-        jax.ShapeDtypeStruct(blocks.shape, f32),
-        [pltpu.SemaphoreType.DMA((n,)), pltpu.SemaphoreType.DMA((n,))],
-        blocks,
-        params=pltpu.CompilerParams(collective_id=number, has_side_effects=True),
-    )
 
 
 def halo_kernel(n, moves, source, *refs):
@@ -560,13 +644,43 @@
     )(*args)
 
 
-def dft_table(n):
-    k = np.arange(n)
-    angle = 2.0 * np.pi / n * ((k[:, None] * k[None, :]) % n)
-    full = np.concatenate([np.cos(angle), np.sin(angle)], axis=0).astype(np.float32)
+def wide(full):
+    full = full.astype(np.float32)
     hi = full.astype(jnp.bfloat16)
     lo = (full - hi.astype(np.float32)).astype(jnp.bfloat16)
-    return np.concatenate([hi, hi, lo], axis=1)
+    return jnp.asarray(np.concatenate([hi, hi, lo], axis=1))
+
+
+def hartley(n, offset=0):
+    k = np.arange(n)
+    angle = 2.0 * np.pi / n * ((k[:, None] * (k[None, :] - offset)) % n)
+    return (np.cos(angle) + np.sin(angle)) / np.sqrt(n)
+
+
+def decay_tables(n, planes):
+    wave = 4.0 * np.sin(np.pi * np.arange(n) / n) ** 2
+    p = (wave[:, None] + wave[None, :]).reshape(-1)
+    p[0] = 1.0
+    mu = 1.0 + 0.5 * p - np.sqrt(p + 0.25 * p * p)
+    weight = top_momentum / (1.0 / mu - mu)
+    close = 1.0 / (1.0 - mu ** (2 * planes))
+    rows = np.stack([mu, weight, close, close * mu**planes])
+    rows[:, 0] = 0.0
+    rows = np.broadcast_to(rows[:, None, :], (4, 8, n * n)).astype(np.float32)
+    return jnp.asarray(rows[0]), jnp.asarray(rows[1]), jnp.asarray(rows[2:])
+
+
+def zero_tables(n, planes):
+    d = np.arange(n)
+    green = top_momentum * ((n * n - 1.0) / (12.0 * n) - d * (n - d) / (2.0 * n))
+    y = np.arange(planes)
+    outs = []
+    for shift in (0, planes):
+        small = green[(y[:, None] - y[None, :] + shift) % n]
+        full = np.zeros((LANES, LANES), np.float32)
+        full[: 4 * planes, : 4 * planes] = np.kron(small, np.eye(4))
+        outs.append(jnp.asarray(full))
+    return outs
 
 
 def body(links):
@@ -579,7 +693,6 @@
     shape = lambda *s: jax.ShapeDtypeStruct(s, f32)
 
 
-    table = jnp.asarray(dft_table(n))
     site = jnp.arange(local, dtype=jnp.int32)
     coords = jnp.stack([site % n, (me * q + site // n - 1) % n])
     coords = jnp.broadcast_to(coords[:, None, :], (2, slices, local))
@@ -598,31 +711,29 @@
         (shape(8, slices, plane), shape(8, slices, LANES), shape(8, slices, LANES)),
         2,
     )
-    head = -(-(local // 2) // (8 * n)) * 8 * n
-    qh = head // n
-    nsplit = 2
-    kept = packed_rows(q, n * nsplit // devices)
-    spread, theta = call(
-        functools.partial(spread_kernel, n, head, nsplit, q),
-        (shape(devices, kept, LANES), shape(slices, LANES)),
-        [pltpu.VMEM((LANES, head), f32), pltpu.VMEM((head, LANES), f32), pltpu.VMEM((head, LANES), f32)],
-        alg, y_rim, z_below, z_above, coords, table,
-    )
-    planes = exchange(spread, devices, 3)
-    wave_np = (4.0 * np.sin(np.pi * np.arange(n) / n) ** 2).astype(np.float32)
-    wave = jnp.asarray(np.ascontiguousarray(np.broadcast_to(wave_np[:, None], (n, LANES))))
-    smoothed = call(
-        functools.partial(plane_kernel, n, nsplit),
-        shape(devices, kept, LANES),
-        [pltpu.VMEM((plane, LANES), f32), pltpu.VMEM((plane, LANES), f32)],
-        planes, wave, table,
-    )
-    back = exchange(smoothed, devices, 4)
+    group = devices // 2
+    planes = n // 2
+    nb = local // LANES
+    assert group * 4 == 8 * slices and nb % UNITS == 0
+    dma = lambda *s: pltpu.SemaphoreType.DMA(s)
+    fields, theta = call(
+        functools.partial(spread_kernel, n, group),
+        (shape(group * nb + 1, 4, LANES), shape(slices, LANES)),
+        [pltpu.VMEM((group, nb, 4, LANES), f32), dma(UNITS, group), dma(UNITS, group), dma(group), dma(1)],
+        alg, y_rim, z_below, z_above, coords,
+        params=pltpu.CompilerParams(collective_id=3, has_side_effects=True, vmem_limit_bytes=60 * 1024 * 1024),
+    )
+    vm = lambda *s: pltpu.VMEM(s, f32)
     smooth = call(
-        functools.partial(gather_kernel, n, head, nsplit),
+        functools.partial(solve_kernel, n, group),
         shape(8, slices, local),
-        [pltpu.VMEM((head, LANES), f32), pltpu.VMEM((head, LANES), f32)],
-        back, table,
+        [
+            vm(plane, LANES), vm(plane, LANES), vm(4 * planes, plane), vm(8, plane), vm(8, plane),
+            vm(8, LANES), vm(8, LANES), vm(group * nb + 1, 4, LANES), vm(group, nb, 4, LANES), vm(group, 1, 4, LANES),
+            dma(PIECES + 1), dma(PIECES + 1), dma(UNITS, group), dma(UNITS, group), dma(1), dma(group),
+        ],
+        fields, *decay_tables(n, planes), wide(hartley(n)), wide(hartley(n, 1)), wide(hartley(n, 1).T), *zero_tables(n, planes),
+        params=pltpu.CompilerParams(collective_id=4, has_side_effects=True, vmem_limit_bytes=60 * 1024 * 1024),
     )
     above, below = halos(
         smooth,

time: 149 us -> 116 us (0.78)
  Pallas kernels: 134 us -> 102 us
    pallas_call x10 -> x7, Pallas kernels: 134 us -> 102 us  [call(): pl.pallas_call(kernel, out_shape=out_shape, in_specs=[VM] * len(args), ou...]
where the time goes in v1:
time: 116 us
  Pallas kernels  102 us (88%)
  local copies, waits for them, and re-layouts  11.7 us (10%)
  between operations  2.39 us (2%)
    pallas_call x7, Pallas kernels, call(): pl.pallas_call(kernel, out_shape=out_shape, in_specs=[VM] * len(args), ou...  102 us
    unnamed x5, local copies, waits for them, and re-layouts  11 us

profile of v1, /device:TPU:0, one launch (start us, length us, event | category | flops | bytes accessed | tf_op | source)
XLA Modules:
  0.0 116.0 jit_solution(5527995218785773217)
XLA Ops:
  0.6 0.1 and_select_fusion
  0.8 0.7 broadcast_in_dim.2.coords
  1.5 4.3 %copy.15 = f32[8,3,2,3,2,3456]{5,0,4,3,2,1:T(8,128)} copy(f32[8,3,2,3,2,3456]{5,4,3,2,1,0:T(2,128)} %param.9) | data formatting | bytes 7962624 | tf_op args[0]
  5.8 4.4 %shard_map.112.source.alg = f32[3,8,8,3456]{3,2,1,0:T(8,128)} custom-call(f32[3,2,3,2,8,3456]{5,4,3,2,1,0:T(8,128)} %bitcast.6), custom_call_target="tpu_custom_call" | custom-call | tf_op jit(solution)/shard_map/pallas_call | solution.py:637
  10.3 17.6 %shard_map.113 = (f32[8,8,2304]{2,1,0:T(8,128)}, f32[8,8,128]{2,1,0:T(8,128)}, f32[8,8,128]{2,1,0:T(8,128)}) custom-call(f32[3,8,8,3456]{3,2,1,0:T(8,128)} %shard_map.112.source.alg), custom_call_target="tpu_custom_call" | custom-call | tf_op jit(solution)/shard_map/pallas_call | solution.py:637
  27.9 17.5 %shard_map.114 = (f32[433,4,128]{2,1,0:T(4,128)}, f32[8,128]{1,0:T(8,128)}) custom-call(f32[3,8,8,3456]{3,2,1,0:T(8,128)} %shard_map.112.source.alg, f32[8,8,2304]{2,1,0:T(8,128)} %get-tuple-element.14.y_rim, f32[8,8,128]{2,1,0:T(8,128)} %get-tuple-element.15.z_below, f32[8,8,128]{2,1,0:T(8,128)} %get-tuple-element.16.z_above, ...), custom_call_target="tpu_custom_call" | custom-call | tf_op jit(solution)/shard_map/pallas_call | solution.py:637
  45.4 28.0 %shard_map.115.source.smooth = f32[8,8,3456]{2,1,0:T(8,128)} custom-call(f32[433,4,128]{2,1,0:T(4,128)} %get-tuple-element.17.fields, f32[8,2304]{1,0:T(8,128)} %constant.47.clone.decay, f32[8,2304]{1,0:T(8,128)} %constant.48.clone.weight, f32[2,8,2304]{2,1,0:T(8,128)} %constant.49.clone.close, bf16[48,144]{1,0:T(8,128)(2,1)} %constant.50.clone.x_table, ...), custom_call_target="tpu_custom_call" | custom-call | tf_op jit(solution)/shard_map/pallas_call | solution.py:637
  73.4 11.9 %shard_map.116 = (f32[8,8,2304]{2,1,0:T(8,128)}, f32[8,8,128]{2,1,0:T(8,128)}) custom-call(f32[8,8,3456]{2,1,0:T(8,128)} %shard_map.115.source.smooth), custom_call_target="tpu_custom_call" | custom-call | tf_op jit(solution)/shard_map/pallas_call | solution.py:637
  85.3 12.1 %shard_map.117 = (f32[3,2,3,2,8,3456]{5,4,3,2,1,0:T(8,128)}, f32[8,128]{1,0:T(8,128)}) custom-call(f32[3,2,3,2,8,3456]{5,4,3,2,1,0:T(8,128)} %bitcast.7, f32[8,8,3456]{2,1,0:T(8,128)} %shard_map.115.source.smooth, f32[8,8,2304]{2,1,0:T(8,128)} %get-tuple-element.18.above, f32[8,8,128]{2,1,0:T(8,128)} %get-tuple-element.19.below, ...), custom_call_target="tpu_custom_call" | custom-call | tf_op jit(solution)/shard_map/pallas_call | solution.py:637
  97.4 10.2 %shard_map.118 = (f32[1,1]{1,0:T(1,128)}, f32[1,8]{1,0:T(1,128)}) custom-call(f32[8,128]{1,0:T(8,128)} %get-tuple-element.21.theta, f32[8,128]{1,0:T(8,128)} %get-tuple-element.22.deficit), custom_call_target="tpu_custom_call" | custom-call | tf_op jit(solution)/shard_map/pallas_call | solution.py:637
  107.6 0.0 copy-start
  107.7 6.1 %copy.13 = f32[8,3,2,3,2,3456]{5,4,3,2,1,0:T(2,128)} copy(f32[8,3,2,3,2,3456]{5,0,4,3,2,1:T(8,128)} %bitcast.8) | data formatting | bytes 7962624
  114.3 0.0 copy-done
  114.3 0.5 copy.19
  (1 shorter events, 0.0 us)
Async XLA Ops:
  107.6 6.7 %copy-start = (f32[1,8]{1,0:T(1,128)S(1)}, f32[1,8]{1,0:T(1,128)}, u32[]{:S(2)}) copy-start(f32[1,8]{1,0:T(1,128)} %get-tuple-element.24) | copy-start | bytes 100

commit v2 on v1

--- a/solution.py
+++ b/solution.py
@@ -13,6 +13,7 @@
 LANES = 128
 UNITS = 3
 PIECES = 6
+LINK_MB = 24
 
 root_three = math.sqrt(3.0)
 step_size = 0.08
@@ -22,7 +23,6 @@
 bf16 = jnp.bfloat16
 MESH = pl.DeviceIdType.MESH
 VM = pl.BlockSpec(memory_space=pltpu.VMEM)
-PARAMS = pltpu.CompilerParams(vmem_limit_bytes=60 * 1024 * 1024)
 
 
 def cmul(p, q):
@@ -127,20 +127,36 @@
     return lax.broadcasted_iota(jnp.int32, (rows, LANES), 1)
 
 
-def load_link(ref, d, sl):
-    rows = [[(ref[d, r, c, 0, :, sl], ref[d, r, c, 1, :, sl]) for c in range(3)] for r in range(2)]
+def rows_of(slices, d, r, c, p):
+    return pl.ds((d * 2 + r) * 6 + c * 2 + p, slices, stride=36)
+
+
+def flat_block(ref, k):
+    return ref.at[k].reshape(ref.shape[1] * 36, LANES)
+
+
+def load_link(ref, slices, d):
+    rows = [[tuple(ref[rows_of(slices, d, r, c, p), :] for p in range(2)) for c in range(3)] for r in range(2)]
     return rows + [cross_conj(rows[0], rows[1])]
 
 
-def algebra_kernel(links, out):
-    def step(k, carry):
-        sl = block(k)
-        for d in range(3):
-            for a, v in enumerate(algebra_of(load_link(links, d, sl))):
-                out[d, a, :, sl] = v
-        return carry
-
-    lax.fori_loop(0, links.shape[-1] // LANES, step, 0)
+def site_of(k, extent):
+    start = k * LANES
+    shifted = lane_ids() + lax.rem(start, extent)
+    wraps = sum((shifted >= extent * i).astype(jnp.int32) for i in range(1, (LANES + extent - 1) // extent + 1))
+    return shifted - extent * wraps, lax.div(start, extent) + wraps
+
+
+def at_z(row, z, me, rows, extent):
+    first = lax.rem(extent + z + 1 - lax.rem(me * rows, extent), extent)
+    hit = row == first
+    for i in range(1, -(-rows // extent)):
+        hit = hit | (row == first + i * extent)
+    return hit
+
+
+def fetch_block(links, held, sem, k, start=0):
+    return pltpu.make_async_copy(links.at[:, :, :, :, :, pl.ds(k * LANES, LANES)], held.at[k - start], sem.at[k])
 
 
 def split3(x):
@@ -167,35 +183,93 @@
 
 
 def spread_kernel(
-    extent, group, alg, y_rim, z_below, z_above, coords, out, theta, mine, send_sem, recv_sem, edge_send, edge_recv
+    extent, group, links, out, theta, *refs
 ):
-    nb = alg.shape[-1] // LANES
-    yb = y_rim.shape[-1] // LANES
-    half = alg.shape[2] // 2
-    third = nb // UNITS
+    parts = refs[: UNITS + 1]
+    (
+        alg, y_rim, z_below, z_above, mine,
+        load_sem, halo_send, halo_recv, send_sem, recv_sem, edge_send, edge_recv,
+    ) = refs[UNITS + 1 :]
+    n = 2 * group
+    nb, slices = mine.shape[1], alg.shape[2]
+    yb = extent * extent // LANES
+    half = slices // 2
+    unit = nb // UNITS
+    q = nb * LANES // extent
+    mid = (extent // 2) * extent
     lane = lane_ids()
     me = lax.axis_index("space")
     place = lax.rem(me, group)
     base = me - place
     beyond = group - base
+    ahead, behind = lax.rem(me + 1, n), lax.rem(me + n - 1, n)
+    spans = [(0, 1)] + [(i * unit, (i + 1) * unit) for i in range(1, UNITS)] + [(1, unit)]
+    loads = [[fetch_block(links, held, load_sem, k, a) for k in range(a, b)] for (a, b), held in zip(spans, parts)]
+    for copy in sum(loads, []):
+        copy.start()
     barrier = greet([base + flip(place, i, group) for i in range(1, group)] + [beyond + i for i in range(group)])
 
-    def step(k, total):
+    def algebra(i):
+        start, stop = spans[i]
+
+        def step(k, carry):
+            flat = flat_block(parts[i], k - start)
+            for d in range(3):
+                for a, v in enumerate(algebra_of(load_link(flat, slices, d))):
+                    alg[d, a, :, block(k)] = v
+            return carry
+
+        for copy in loads[i]:
+            copy.wait()
+        lax.fori_loop(start, stop, step, 0)
+
+    def halo(i, source, dest, other):
+        return pltpu.make_async_remote_copy(
+            src_ref=source,
+            dst_ref=dest,
+            send_sem=halo_send.at[i],
+            recv_sem=halo_recv.at[i],
+            device_id={"space": other},
+            device_id_type=MESH,
+        )
+
+    def span(start, size):
+        return pl.ds(pl.multiple_of(start * LANES, LANES), size * LANES)
+
+    first = nb - yb
+    rims = [
+        halo(i, alg.at[1, :, :, span(first + i * unit, unit)], y_rim.at[:, :, span(i * unit, unit)], ahead)
+        for i in range(yb // unit)
+    ]
+    below_copy = halo(len(rims), alg.at[2, :, :, span(nb - 1, 1)], z_below, ahead)
+    odd = lax.rem(me, 2)
+    above_copy = halo(len(rims) + 1, alg.at[2, :, :, span(odd * (mid // LANES), 1)], z_above, behind)
+
+    algebra(0)
+    algebra(1)
+    pl.semaphore_wait(barrier, n - 1)
+    above_copy.start()
+    rims[0].start()
+    for i in range(1, len(rims)):
+        algebra(1 + i)
+        if i == len(rims) - 1:
+            below_copy.start()
+        rims[i].start()
+    algebra(UNITS)
+
+    def step(from_rim, k, total):
         sl = block(k)
         before = block(jnp.maximum(k - 1, 0))
         after = block(jnp.minimum(k + 1, nb - 1))
-        edge_x = coords[0, :, sl] == 0
-        edge_z = coords[1, :, sl] == 0
+        x_at, row = site_of(k, extent)
+        edge_x = x_at == 0
+        edge_z = at_z(row, 0, me, q, extent)
         for a in range(8):
             x, y, z = alg[0, a, :, sl], alg[1, a, :, sl], alg[2, a, :, sl]
             near = pltpu.roll(jnp.where(lane == LANES - 1, alg[0, a, :, before], x), 1, 1)
             far = pltpu.roll(jnp.where(lane < extent - 1, alg[0, a, :, after], x), LANES - extent + 1, 1)
             bx = jnp.where(edge_x, far, near)
-            by = jnp.where(
-                k < yb,
-                y_rim[a, :, block(jnp.minimum(k, yb - 1))],
-                alg[1, a, :, block(jnp.maximum(k - yb, 0))],
-            )
+            by = y_rim[a, :, sl] if from_rim else alg[1, a, :, block(k - yb)]
             prev = jnp.where(k == 0, z_below[a], alg[2, a, :, before])
             near = pltpu.roll(jnp.where(lane >= LANES - extent, prev, z), extent, 1)
             far = pltpu.roll(jnp.where(k == 0, alg[2, a, :, block(yb)], z_above[a]), extent, 1)
@@ -218,10 +292,13 @@
 
     total = jnp.zeros((8, LANES), f32)
     copies = []
-    for c in range(UNITS):
-        total = lax.fori_loop(c * third, (c + 1) * third, step, total)
+    above_copy.wait_recv()
+    below_copy.wait_recv()
+    for c in [UNITS - 1] + list(range(UNITS - 1)):
+        if c < len(rims):
+            rims[c].wait_recv()
+        total = lax.fori_loop(c * unit, (c + 1) * unit, functools.partial(step, c < len(rims)), total)
         if c == 0:
-            pl.semaphore_wait(barrier, 2 * group - 1)
 
             @pl.when(place == 0)
             def _():
@@ -231,8 +308,8 @@
         for i in reversed(range(1, group)):
             other = flip(place, i, group)
             copy = pltpu.make_async_remote_copy(
-                src_ref=mine.at[other, pl.ds(c * third, third)],
-                dst_ref=out.at[pl.ds(place * nb + c * third, third)],
+                src_ref=mine.at[other, pl.ds(c * unit, unit)],
+                dst_ref=out.at[pl.ds(place * nb + c * unit, unit)],
                 send_sem=send_sem.at[c, i],
                 recv_sem=recv_sem.at[c, i],
                 device_id={"space": base + other},
@@ -247,6 +324,8 @@
         return carry
 
     lax.fori_loop(0, nb, keep, 0)
+    for copy in rims + [below_copy, above_copy]:
+        copy.wait_send()
     for copy in copies:
         copy.wait()
     edge_copy(0).wait_recv()
@@ -491,10 +570,23 @@
             smooth[a, :, 0:LANES] = jnp.where(lane_ids() < n, row, smooth[a, :, 0:LANES])
 
 
-def link_kernel(extent, links, smooth, above, below, coords, out, deficit, rot):
-    nb = smooth.shape[-1] // LANES
-    yb = above.shape[-1] // LANES
+def link_kernel(
+    extent, scales, links, smooth, theta, done, out_theta, out_deficit,
+    held, above, below, rot, mine, sums, load_sem, halo_send, halo_recv, send_sem, recv_sem,
+):
+    nb, slices = held.shape[0], held.shape[1]
+    n = sums.shape[0]
+    yb = extent * extent // LANES
+    unit = nb // UNITS
+    q = nb * LANES // extent
+    mid = (extent // 2) * extent
     lane = lane_ids()
+    me = lax.axis_index("space")
+    ahead, behind = lax.rem(me + 1, n), lax.rem(me + n - 1, n)
+    loads = [fetch_block(links, held, load_sem, k) for k in range(nb)]
+    for copy in loads:
+        copy.start()
+    barrier = greet([lax.rem(me + i, n) for i in range(1, n)])
 
     def rotate(values, sl):
         g = rotation_of(values)
@@ -511,17 +603,41 @@
         rotate([above[a, :, block(k)] for a in range(8)], block(nb + k))
         return carry
 
-    lax.fori_loop(0, nb, rotate_own, 0)
-    lax.fori_loop(0, yb, rotate_above, 0)
-    rotate([below[a] for a in range(8)], block(nb + yb))
-
-    def step(k, total):
+    def halo(i, source, dest, other):
+        return pltpu.make_async_remote_copy(
+            src_ref=source,
+            dst_ref=dest,
+            send_sem=halo_send.at[i],
+            recv_sem=halo_recv.at[i],
+            device_id={"space": other},
+            device_id_type=MESH,
+        )
+
+    def span(start, size):
+        return pl.ds(pl.multiple_of(start * LANES, LANES), size * LANES)
+
+    odd = lax.rem(me, 2)
+    pick = yb - odd * (yb - mid // LANES)
+    below_copy = halo(0, smooth.at[:, :, span(pick, 1)], below, ahead)
+    rims = [
+        halo(1 + i, smooth.at[:, :, span(i * unit, unit)], above.at[:, :, span(i * unit, unit)], behind)
+        for i in range(yb // unit)
+    ]
+
+    lax.fori_loop(0, unit, rotate_own, 0)
+    pl.semaphore_wait(barrier, n - 1)
+    for copy in [below_copy] + rims:
+        copy.start()
+    lax.fori_loop(unit, nb, rotate_own, 0)
+
+    def step(which, k, total):
         sl = block(k)
         before = block(jnp.maximum(k - 1, 0))
         after = block(k + 1)
         wrap = block(jnp.where(k == yb, 0, nb + yb))
-        edge_x = coords[0, :, sl] == extent - 1
-        edge_z = coords[1, :, sl] == extent - 1
+        x_at, row = site_of(k, extent)
+        edge_x = x_at == extent - 1
+        edge_z = at_z(row, extent - 1, me, q, extent)
 
         def ahead_x(e):
             cur = rot[e, :, sl]
@@ -538,84 +654,52 @@
             far = pltpu.roll(rot[e, :, wrap], LANES - extent, 1)
             return jnp.where(edge_z, far, near)
 
-        for d, ahead in enumerate((ahead_x, ahead_y, ahead_z)):
-            u = load_link(links, d, sl)
+        flat_out = flat_block(done, k)
+        for d in which:
+            forward = (ahead_x, ahead_y, ahead_z)[d]
+            u = load_link(flat_block(held, k), slices, d)
             own = [[(rot[6 * i + 2 * j, :, sl], rot[6 * i + 2 * j + 1, :, sl]) for j in range(3)] for i in range(3)]
             left = [
                 [dot_row(own[i], [u[k2][j] for k2 in range(3)], cmul) for j in range(3)]
                 for i in range(3)
             ]
             for j in range(3):
-                row = [(ahead(6 * j + 2 * c), ahead(6 * j + 2 * c + 1)) for c in range(3)]
+                row3 = [(forward(6 * j + 2 * c), forward(6 * j + 2 * c + 1)) for c in range(3)]
                 for i in range(2):
-                    v = dot_row(left[i], row, mul_conj)
-                    out[d, i, j, 0, :, sl] = v[0]
-                    out[d, i, j, 1, :, sl] = v[1]
+                    v = dot_row(left[i], row3, mul_conj)
+                    flat_out[rows_of(slices, d, i, j, 0), :] = v[0]
+                    flat_out[rows_of(slices, d, i, j, 1), :] = v[1]
                     if i == j:
                         total = total + (1.0 - v[0])
                 if j == 2:
-                    total = total + (1.0 - dot_row(left[2], row, mul_conj)[0])
+                    total = total + (1.0 - dot_row(left[2], row3, mul_conj)[0])
         return total
 
-    deficit[...] = lax.fori_loop(0, nb, step, jnp.zeros((8, LANES), f32))
-
-
-def greet(others):
-    barrier = pltpu.get_barrier_semaphore()
-    for other in others:
-        pl.semaphore_signal(barrier, inc=1, device_id={"space": other}, device_id_type=MESH)
-    return barrier
-
-
-def halo_kernel(n, moves, source, *refs):
-    outs, (send_sem, recv_sem) = refs[:-2], refs[-2:]
-    me = lax.axis_index("space")
-    ahead, behind = lax.rem(me + 1, n), lax.rem(me + n - 1, n)
-    barrier = greet([ahead, behind])
-    pl.semaphore_wait(barrier, 2)
-    odd = lax.rem(me, 2)
-    copies = []
-    for i, (direction, select) in enumerate(moves):
-        copy = pltpu.make_async_remote_copy(
-            src_ref=select(source, odd),
-            dst_ref=outs[i],
-            send_sem=send_sem.at[i],
-            recv_sem=recv_sem.at[i],
-            device_id={"space": ahead if direction > 0 else behind},
-            device_id_type=MESH,
-        )
-        copy.start()
-        copies.append(copy)
-    for copy in copies:
+    for copy in loads:
         copy.wait()
-
-
-def halos(source, n, moves, shapes, number):
-    count = len(moves)
-    return call(
-        functools.partial(halo_kernel, n, moves),
-        shapes,
-        [pltpu.SemaphoreType.DMA((count,)), pltpu.SemaphoreType.DMA((count,))],
-        source,
-        params=pltpu.CompilerParams(collective_id=number, has_side_effects=True),
+    below_copy.wait_recv()
+    rotate([below[a] for a in range(8)], block(nb + yb))
+    total = jnp.zeros((8, LANES), f32)
+    total = lax.fori_loop(0, nb - yb, functools.partial(step, (0, 1, 2)), total)
+    total = lax.fori_loop(nb - yb, nb - 1, functools.partial(step, (0, 2)), total)
+    for i, copy in enumerate(rims):
+        copy.wait_recv()
+        lax.fori_loop(i * unit, (i + 1) * unit, rotate_above, 0)
+    total = lax.fori_loop(nb - yb, nb - 1, functools.partial(step, (1,)), total)
+    total = lax.fori_loop(nb - 1, nb, functools.partial(step, (0, 1, 2)), total)
+
+    wide_lane = lane_ids(slices)
+    t = jnp.sum(jnp.sum(theta[...], axis=1, keepdims=True), axis=0, keepdims=True)
+    d = jnp.sum(total, axis=1, keepdims=True)
+    own_row = lax.broadcasted_iota(jnp.int32, (slices, LANES), 0)
+    mine[...] = jnp.where(
+        wide_lane == own_row, d, jnp.where(wide_lane == slices, jnp.where(own_row == 0, t, 0.0), 0.0)
     )
-
-
-def sum_kernel(n, scales, theta, deficit, out_theta, out_deficit, mine, held, send_sem, recv_sem):
-    me = lax.axis_index("space")
-    barrier = greet([lax.rem(me + i, n) for i in range(1, n)])
-    slices = deficit.shape[0]
-    lane = lane_ids(slices)
-    t = jnp.sum(jnp.sum(theta[...], axis=1, keepdims=True), axis=0, keepdims=True)
-    d = jnp.sum(deficit[...], axis=1, keepdims=True)
-    own = lax.broadcasted_iota(jnp.int32, (slices, LANES), 0)
-    mine[...] = jnp.where(lane == own, d, jnp.where(lane == slices, jnp.where(own == 0, t, 0.0), 0.0))
-    pl.semaphore_wait(barrier, n - 1)
     copies = []
     for i in range(1, n):
         copy = pltpu.make_async_remote_copy(
             src_ref=mine,
-            dst_ref=held.at[i],
+            dst_ref=sums.at[i],
             send_sem=send_sem.at[i],
             recv_sem=recv_sem.at[i],
             device_id={"space": lax.rem(me + i, n)},
@@ -623,24 +707,49 @@
         )
         copy.start()
         copies.append(copy)
+    for copy in [below_copy] + rims:
+        copy.wait_send()
     for copy in copies:
         copy.wait()
     total = mine[...]
     for i in range(1, n):
-        total = total + held[i]
+        total = total + sums[i]
     row = jnp.sum(total, axis=0, keepdims=True)
     out_deficit[...] = row[:, :slices] * scales[1]
     out_theta[...] = row[:, slices : slices + 1] * scales[0]
 
 
-def call(kernel, out_shape, scratch, *args, params=PARAMS):
+def place_kernel(blocks, out, sem):
+    copies = [
+        pltpu.make_async_copy(blocks.at[k], out.at[:, :, :, :, :, pl.ds(k * LANES, LANES)], sem.at[k])
+        for k in range(blocks.shape[0])
+    ]
+    for copy in copies:
+        copy.start()
+    for copy in copies:
+        copy.wait()
+
+
+def greet(others):
+    barrier = pltpu.get_barrier_semaphore()
+    for other in others:
+        pl.semaphore_signal(barrier, inc=1, device_id={"space": other}, device_id_type=MESH)
+    return barrier
+
+
+ANY = pl.BlockSpec(memory_space=pl.ANY)
+
+
+def call(kernel, number, out_shape, scratch, *args, in_specs=None, out_specs=None, limit=60):
     return pl.pallas_call(
         kernel,
         out_shape=out_shape,
-        in_specs=[VM] * len(args),
-        out_specs=jax.tree.map(lambda _: VM, out_shape),
+        in_specs=in_specs or [VM] * len(args),
+        out_specs=out_specs or jax.tree.map(lambda _: VM, out_shape),
         scratch_shapes=scratch,
-        compiler_params=params,
+        compiler_params=pltpu.CompilerParams(
+            collective_id=number, has_side_effects=True, vmem_limit_bytes=limit * 1024 * 1024
+        ),
     )(*args)
 
 
@@ -688,44 +797,31 @@
     slices, local = links.shape[0], links.shape[-1]
     devices = lax.axis_size("space")
     plane = n * n
-    q = local // n
-    me = lax.axis_index("space")
     shape = lambda *s: jax.ShapeDtypeStruct(s, f32)
-
-
-    site = jnp.arange(local, dtype=jnp.int32)
-    coords = jnp.stack([site % n, (me * q + site // n - 1) % n])
-    coords = jnp.broadcast_to(coords[:, None, :], (2, slices, local))
-    across = jnp.transpose(links, (1, 2, 3, 4, 0, 5))
-    alg = call(algebra_kernel, shape(3, 8, slices, local), [], across)
-    mid = (n // 2) * n
-    side = lambda start: pl.ds(pl.multiple_of(start, LANES), LANES)
-    y_rim, z_below, z_above = halos(
-        alg,
-        devices,
-        [
-            (1, lambda r, odd: r.at[1, :, :, local - plane :]),
-            (1, lambda r, odd: r.at[2, :, :, local - LANES :]),
-            (-1, lambda r, odd: r.at[2, :, :, side(odd * mid)]),
-        ],
-        (shape(8, slices, plane), shape(8, slices, LANES), shape(8, slices, LANES)),
-        2,
-    )
+    vm = lambda *s: pltpu.VMEM(s, f32)
+    dma = lambda *s: pltpu.SemaphoreType.DMA(s)
     group = devices // 2
     planes = n // 2
     nb = local // LANES
-    assert group * 4 == 8 * slices and nb % UNITS == 0
-    dma = lambda *s: pltpu.SemaphoreType.DMA(s)
+    assert group * 4 == 8 * slices and nb % UNITS == 0 and plane % (nb // UNITS * LANES) == 0
+    rims = plane // (nb // UNITS * LANES)
+    blocks = (nb, slices, 3, 2, 3, 2, LANES)
     fields, theta = call(
         functools.partial(spread_kernel, n, group),
+        1,
         (shape(group * nb + 1, 4, LANES), shape(slices, LANES)),
-        [pltpu.VMEM((group, nb, 4, LANES), f32), dma(UNITS, group), dma(UNITS, group), dma(group), dma(1)],
-        alg, y_rim, z_below, z_above, coords,
-        params=pltpu.CompilerParams(collective_id=3, has_side_effects=True, vmem_limit_bytes=60 * 1024 * 1024),
+        [
+            *[vm(count, *blocks[1:]) for count in [1] + [nb // UNITS] * (UNITS - 1) + [nb // UNITS - 1]],
+            vm(3, 8, slices, local), vm(8, slices, plane), vm(8, slices, LANES), vm(8, slices, LANES),
+            vm(group, nb, 4, LANES), dma(nb), dma(rims + 2), dma(rims + 2),
+            dma(UNITS, group), dma(UNITS, group), dma(group), dma(1),
+        ],
+        links,
+        in_specs=[ANY],
     )
-    vm = lambda *s: pltpu.VMEM(s, f32)
     smooth = call(
         functools.partial(solve_kernel, n, group),
+        2,
         shape(8, slices, local),
         [
             vm(plane, LANES), vm(plane, LANES), vm(4 * planes, plane), vm(8, plane), vm(8, plane),
@@ -733,39 +829,30 @@
             dma(PIECES + 1), dma(PIECES + 1), dma(UNITS, group), dma(UNITS, group), dma(1), dma(group),
         ],
         fields, *decay_tables(n, planes), wide(hartley(n)), wide(hartley(n, 1)), wide(hartley(n, 1).T), *zero_tables(n, planes),
-        params=pltpu.CompilerParams(collective_id=4, has_side_effects=True, vmem_limit_bytes=60 * 1024 * 1024),
     )
-    above, below = halos(
-        smooth,
-        devices,
-        [
-            (-1, lambda r, odd: r.at[:, :, :plane]),
-            (1, lambda r, odd: r.at[:, :, side(plane - odd * (plane - mid))]),
-        ],
-        (shape(8, slices, plane), shape(8, slices, LANES)),
-        5,
-    )
-    turned, deficit = call(
-        functools.partial(link_kernel, n),
-        (shape(3, 2, 3, 2, slices, local), shape(slices, LANES)),
-        [pltpu.VMEM((18, slices, local + plane + LANES), f32)],
-        across, smooth, above, below, coords,
-    )
-    new_links = jnp.transpose(turned, (4, 0, 1, 2, 3, 5))
     times = lax.axis_size("tm")
     scales = (1.0 / (slices * times * n**3), 1.0 / n**3)
-    total, shares = call(
-        functools.partial(sum_kernel, devices, scales),
-        (shape(1, 1), shape(1, slices)),
+    placed, total, shares = call(
+        functools.partial(link_kernel, n, scales),
+        3,
+        (shape(*blocks), shape(1, 1), shape(1, slices)),
         [
-            pltpu.VMEM((slices, LANES), f32),
-            pltpu.VMEM((devices, slices, LANES), f32),
-            pltpu.SemaphoreType.DMA((devices,)),
-            pltpu.SemaphoreType.DMA((devices,)),
+            vm(*blocks), vm(8, slices, plane), vm(8, slices, LANES), vm(18, slices, local + plane + LANES),
+            vm(slices, LANES), vm(devices, slices, LANES), dma(nb), dma(rims + 1), dma(rims + 1),
+            dma(devices), dma(devices),
         ],
-        theta, deficit,
-        params=pltpu.CompilerParams(collective_id=1, has_side_effects=True),
+        links, smooth, theta,
+        in_specs=[ANY, VM, VM],
+        limit=LINK_MB,
     )
+    new_links = pl.pallas_call(
+        place_kernel,
+        out_shape=shape(*links.shape),
+        in_specs=[VM],
+        out_specs=ANY,
+        scratch_shapes=[dma(nb)],
+        compiler_params=pltpu.CompilerParams(vmem_limit_bytes=8 * 1024 * 1024),
+    )(placed)
     total = total.reshape(())
     if times > 1:
         total = lax.psum(total, "tm")

time: 116 us -> 84.9 us (0.73)
  Pallas kernels: 102 us -> 79.8 us
  local copies, waits for them, and re-layouts: 11.7 us -> 2.36 us
    pallas_call x7 -> x4, Pallas kernels: 102 us -> 79.8 us  [the longest x3 77.7 us: call(): pl.pallas_call(kernel, out_shape=out_shape, in_specs=in_specs or [VM] * l...]
    unnamed x5 -> x7, local copies, waits for them, and re-layouts: 11 us -> 2.36 us
where the time goes in v2:
time: 84.9 us; the launch traced here: 84.6 us
  Pallas kernels  79.8 us (94%)
  between operations  2.43 us (3%)
  local copies, waits for them, and re-layouts  2.36 us (3%)
    pallas_call x3, Pallas kernels, call(): pl.pallas_call(kernel, out_shape=out_shape, in_specs=in_specs or [VM] * l...  77.7 us
    unnamed x7, local copies, waits for them, and re-layouts  2.36 us
    pallas_call x1, Pallas kernels, body(): pl.pallas_call(place_kernel, out_shape=shape(*links.shape), in_specs=[VM]...  2.16 us

profile of v2, /device:TPU:0, one launch (start us, length us, event | category | flops | bytes accessed | tf_op | source)
XLA Modules:
  0.0 84.6 jit_solution(15021349121568935308)
XLA Ops:
  0.6 0.0 copy-start
  0.6 28.8 %shard_map.112 = (f32[433,4,128]{2,1,0:T(4,128)}, f32[8,128]{1,0:T(8,128)}) custom-call(f32[8,3,2,3,2,3456]{5,4,3,2,1,0:T(2,128)} %links.3), custom_call_target="tpu_custom_call" | custom-call | tf_op jit(solution)/shard_map/pallas_call | solution.py:744
  29.4 27.5 %shard_map.113.smooth = f32[8,8,3456]{2,1,0:T(8,128)} custom-call(f32[433,4,128]{2,1,0:T(4,128)} %get-tuple-element.8.fields, f32[8,2304]{1,0:T(8,128)} %constant.16.clone.decay, f32[8,2304]{1,0:T(8,128)} %constant.17.clone.weight, f32[2,8,2304]{2,1,0:T(8,128)} %constant.18.clone.close, bf16[48,144]{1,0:T(8,128)(2,1)} %constant.19.clone.x_table, ...), custom_call_target="tpu_custom_call" | custom-call | tf_op jit(solution)/shard_map/pallas_call | solution.py:744
  56.9 0.0 copy-done
  56.9 0.0 copy-start.1
  56.9 1.2 %copy-done.1 = f32[8,8,3456]{2,1,0:T(8,128)S(1)} copy-done((f32[8,8,3456]{2,1,0:T(8,128)S(1)}, f32[8,8,3456]{2,1,0:T(8,128)}, u32[]{:S(2)}) %copy-start.1) | copy-done | bytes 884760
  58.1 0.0 copy-start.2
  58.1 0.7 copy-done.2
  58.8 21.4 %shard_map.114 = (f32[27,8,3,2,3,2,128]{6,5,4,3,2,1,0:T(2,128)S(1)}, f32[1,1]{1,0:T(1,128)}, f32[1,8]{1,0:T(1,128)S(1)}) custom-call(f32[8,3,2,3,2,3456]{5,4,3,2,1,0:T(2,128)S(1)} %copy-done, f32[8,8,3456]{2,1,0:T(8,128)S(1)} %copy-done.1, f32[8,128]{1,0:T(8,128)S(1)} %copy-done.2), custom_call_target="tpu_custom_call" | custom-call | tf_op jit(solution)/shard_map/pallas_call | solution.py:744
  80.2 2.2 %shard_map.115 = f32[8,3,2,3,2,3456]{5,4,3,2,1,0:T(2,128)} custom-call(f32[27,8,3,2,3,2,128]{6,5,4,3,2,1,0:T(2,128)S(1)} %get-tuple-element.10.blocks), custom_call_target="tpu_custom_call" | custom-call | tf_op jit(solution)/shard_map/pallas_call | solution.py:848
  83.0 0.5 copy.15
Async XLA Ops:
  0.6 56.3 %copy-start = (f32[8,3,2,3,2,3456]{5,4,3,2,1,0:T(2,128)S(1)}, f32[8,3,2,3,2,3456]{5,4,3,2,1,0:T(2,128)}, u32[]{:S(2)}) copy-start(f32[8,3,2,3,2,3456]{5,4,3,2,1,0:T(2,128)} %links.3) | copy-start | bytes 11943940
  56.9 1.2 %copy-start.1 = (f32[8,8,3456]{2,1,0:T(8,128)S(1)}, f32[8,8,3456]{2,1,0:T(8,128)}, u32[]{:S(2)}) copy-start(f32[8,8,3456]{2,1,0:T(8,128)} %shard_map.113.smooth) | copy-start | bytes 2654212
  58.1 0.7 copy-start.2

commit v3 on v2

--- a/solution.py
+++ b/solution.py
@@ -3,7 +3,6 @@
 
 import jax
 import jax.numpy as jnp
-import numpy as np
 from jax import lax
 from jax.experimental import pallas as pl
 from jax.experimental.pallas import tpu as pltpu
@@ -13,7 +12,8 @@
 LANES = 128
 UNITS = 3
 PIECES = 6
-LINK_MB = 24
+COST = 10**9
+GAUGE_KB = 50 * 1000
 
 root_three = math.sqrt(3.0)
 step_size = 0.08
@@ -182,15 +182,173 @@
     return other
 
 
-def spread_kernel(
-    extent, group, links, out, theta, *refs
+def iota(shape, axis):
+    return lax.broadcasted_iota(jnp.int32, shape, axis).astype(f32)
+
+
+def divide(v, n):
+    whole = jnp.floor((v + 0.5) * (1.0 / n))
+    return whole, v - n * whole
+
+
+def make_tables(n, planes, wave, tables, zero):
+    shape = (n, 3 * n)
+    row = iota(shape, 0)
+    third, col = divide(iota(shape, 1), n)
+    for i, turn in enumerate([row * col, row * (col + (n - 1.0)), col * (row + (n - 1.0))]):
+        angle = divide(turn, n)[1] * (2.0 * math.pi / n)
+        full = (jnp.cos(angle) + jnp.sin(angle)) * (1.0 / math.sqrt(n))
+        high = full.astype(bf16).astype(f32)
+        tables[i] = jnp.where(third == 2.0, full - high, high).astype(bf16)
+    mode = iota((8, n * n), 1)
+    p = jnp.zeros((8, n * n), f32)
+    for k in divide(mode, n):
+        s = jnp.sin(k * (math.pi / n))
+        p = p + 4.0 * s * s
+    p = jnp.where(mode == 0.0, 1.0, p)
+    root = jnp.sqrt(p + 0.25 * p * p)
+    mu = 1.0 / (1.0 + 0.5 * p + root)
+    power = lax.integer_pow(mu, planes)
+    close = 1.0 / (1.0 - power * power)
+    for i, v in enumerate([mu, (0.5 * top_momentum) / root, close, close * power]):
+        wave[i] = jnp.where(mode == 0.0, 0.0, v)
+    square = (LANES, LANES)
+    source, sub = divide(iota(square, 0), 4)
+    target, lane = divide(iota(square, 1), 4)
+    used = (sub == lane) & (source < planes) & (target < planes)
+    for i in range(2):
+        d = divide(target - source + (n + i * planes * 1.0), n)[1]
+        green = top_momentum * ((n * n - 1.0) / (12.0 * n) - d * (n - d) * (0.5 / n))
+        zero[i] = jnp.where(used, green, 0.0)
+
+
+def link_part(extent, held, smooth, arrive, done, above, below, rot, halo_send, halo_recv, n):
+    nb, slices = held.shape[0], held.shape[1]
+    yb = extent * extent // LANES
+    unit = nb // UNITS
+    q = nb * LANES // extent
+    mid = (extent // 2) * extent
+    lane = lane_ids()
+    me = lax.axis_index("space")
+    ahead, behind = lax.rem(me + 1, n), lax.rem(me + n - 1, n)
+    def rotate(values, sl):
+        g = rotation_of(values)
+        for i in range(3):
+            for j in range(3):
+                for p in range(2):
+                    rot[6 * i + 2 * j + p, :, sl] = g[i][j][p]
+
+    def rotate_own(k, carry):
+        rotate([smooth[a, :, block(k)] for a in range(8)], block(k))
+        return carry
+
+    def rotate_above(k, carry):
+        rotate([above[a, :, block(k)] for a in range(8)], block(nb + k))
+        return carry
+
+    def halo(i, source, dest, other):
+        return pltpu.make_async_remote_copy(
+            src_ref=source,
+            dst_ref=dest,
+            send_sem=halo_send.at[i],
+            recv_sem=halo_recv.at[i],
+            device_id={"space": other},
+            device_id_type=MESH,
+        )
+
+    def span(start, size):
+        return pl.ds(pl.multiple_of(start * LANES, LANES), size * LANES)
+
+    odd = lax.rem(me, 2)
+    pick = yb - odd * (yb - mid // LANES)
+    below_copy = halo(0, smooth.at[:, :, span(pick, 1)], below, ahead)
+    rims = [
+        halo(1 + i, smooth.at[:, :, span(i * unit, unit)], above.at[:, :, span(i * unit, unit)], behind)
+        for i in range(yb // unit)
+    ]
+
+    for v in range(UNITS):
+        arrive(v)
+        lax.fori_loop(v * unit, (v + 1) * unit, rotate_own, 0)
+        if v < len(rims):
+            rims[v].start()
+    below_copy.start()
+
+    def step(which, k, total):
+        sl = block(k)
+        before = block(jnp.maximum(k - 1, 0))
+        after = block(k + 1)
+        wrap = block(jnp.where(k == yb, 0, nb + yb))
+        x_at, row = site_of(k, extent)
+        edge_x = x_at == extent - 1
+        edge_z = at_z(row, extent - 1, me, q, extent)
+
+        def ahead_x(e):
+            cur = rot[e, :, sl]
+            near = pltpu.roll(jnp.where(lane == 0, rot[e, :, after], cur), LANES - 1, 1)
+            far = pltpu.roll(jnp.where(lane >= LANES - extent + 1, rot[e, :, before], cur), extent - 1, 1)
+            return jnp.where(edge_x, far, near)
+
+        def ahead_y(e):
+            return rot[e, :, block(k + yb)]
+
+        def ahead_z(e):
+            cur = rot[e, :, sl]
+            near = pltpu.roll(jnp.where(lane < extent, rot[e, :, after], cur), LANES - extent, 1)
+            far = pltpu.roll(rot[e, :, wrap], LANES - extent, 1)
+            return jnp.where(edge_z, far, near)
+
+        flat_out = flat_block(done, k)
+        for d in which:
+            forward = (ahead_x, ahead_y, ahead_z)[d]
+            u = load_link(flat_block(held, k), slices, d)
+            own = [[(rot[6 * i + 2 * j, :, sl], rot[6 * i + 2 * j + 1, :, sl]) for j in range(3)] for i in range(2)]
+            left = [
+                [dot_row(own[i], [u[k2][j] for k2 in range(3)], cmul) for j in range(3)]
+                for i in range(2)
+            ]
+            made = []
+            for j in range(3):
+                row3 = [(forward(6 * j + 2 * c), forward(6 * j + 2 * c + 1)) for c in range(3)]
+                for i in range(2):
+                    v = dot_row(left[i], row3, mul_conj)
+                    flat_out[rows_of(slices, d, i, j, 0), :] = v[0]
+                    flat_out[rows_of(slices, d, i, j, 1), :] = v[1]
+                    if j < 2:
+                        made.append(v)
+            p00, p10, p01, p11 = made
+            minor = csub(cmul(p00, p11), cmul(p01, p10))[0]
+            total = total + ((1.0 - p00[0]) + (1.0 - p11[0]) + (1.0 - minor))
+        return total
+
+    total = jnp.zeros((8, LANES), f32)
+    total = lax.fori_loop(1, nb - yb, functools.partial(step, (0, 1, 2)), total)
+    below_copy.wait_recv()
+    rotate([below[a] for a in range(8)], block(nb + yb))
+    total = lax.fori_loop(0, 1, functools.partial(step, (0, 1, 2)), total)
+    total = lax.fori_loop(nb - yb, nb - 1, functools.partial(step, (0, 2)), total)
+    for i, copy in enumerate(rims):
+        copy.wait_recv()
+        lax.fori_loop(i * unit, (i + 1) * unit, rotate_above, 0)
+        last = i == len(rims) - 1
+        total = lax.fori_loop(nb - yb + i * unit, nb - yb + (i + 1) * unit - last, functools.partial(step, (1,)), total)
+    total = lax.fori_loop(nb - 1, nb, functools.partial(step, (0, 1, 2)), total)
+    for copy in [below_copy] + rims:
+        copy.wait_send()
+    return total
+
+
+def gauge_kernel(
+    extent, group, scales, links, done, out_theta, out_deficit, *refs
 ):
-    parts = refs[: UNITS + 1]
     (
-        alg, y_rim, z_below, z_above, mine,
-        load_sem, halo_send, halo_recv, send_sem, recv_sem, edge_send, edge_recv,
-    ) = refs[UNITS + 1 :]
-    n = 2 * group
+        held_links, smooth, above, below, rot, sum_row, sums, late_send, late_recv, sum_send, sum_recv,
+        alg, y_rim, z_below, z_above, mine, fields, load_sem, halo_send, halo_recv,
+        in_send_sem, in_recv_sem, in_edge_send, in_edge_recv,
+        wave, tables, zero, one, two, modes, ends, far, mode, far_mode, outgo, held, edge_held,
+        end_send, end_recv, send_sem, recv_sem, edge_send, edge_recv,
+    ) = refs
+    devices = 2 * group
     nb, slices = mine.shape[1], alg.shape[2]
     yb = extent * extent // LANES
     half = slices // 2
@@ -202,24 +360,26 @@
     place = lax.rem(me, group)
     base = me - place
     beyond = group - base
-    ahead, behind = lax.rem(me + 1, n), lax.rem(me + n - 1, n)
-    spans = [(0, 1)] + [(i * unit, (i + 1) * unit) for i in range(1, UNITS)] + [(1, unit)]
-    loads = [[fetch_block(links, held, load_sem, k, a) for k in range(a, b)] for (a, b), held in zip(spans, parts)]
-    for copy in sum(loads, []):
+    ahead, behind = lax.rem(me + 1, devices), lax.rem(me + devices - 1, devices)
+    in_spans = [(0, 1)] + [(i * unit, (i + 1) * unit) for i in range(1, UNITS)] + [(1, unit)]
+    in_loads = [[fetch_block(links, held_links, load_sem, k) for k in range(a, b)] for a, b in in_spans]
+    for copy in sum(in_loads, []):
         copy.start()
     barrier = greet([base + flip(place, i, group) for i in range(1, group)] + [beyond + i for i in range(group)])
 
+    make_tables(extent, extent // 2, wave, tables, zero)
+
     def algebra(i):
-        start, stop = spans[i]
+        start, stop = in_spans[i]
 
         def step(k, carry):
-            flat = flat_block(parts[i], k - start)
+            flat = flat_block(held_links, k)
             for d in range(3):
                 for a, v in enumerate(algebra_of(load_link(flat, slices, d))):
                     alg[d, a, :, block(k)] = v
             return carry
 
-        for copy in loads[i]:
+        for copy in in_loads[i]:
             copy.wait()
         lax.fori_loop(start, stop, step, 0)
 
@@ -247,7 +407,7 @@
 
     algebra(0)
     algebra(1)
-    pl.semaphore_wait(barrier, n - 1)
+    pl.semaphore_wait(barrier, devices - 1)
     above_copy.start()
     rims[0].start()
     for i in range(1, len(rims)):
@@ -280,18 +440,18 @@
             mine[2 * a + 1, k] = b[half:]
         return total
 
-    def edge_copy(i):
+    def in_edge_copy(i):
         return pltpu.make_async_remote_copy(
             src_ref=mine.at[i, pl.ds(0, 1)],
-            dst_ref=out.at[pl.ds(group * nb, 1)],
-            send_sem=edge_send.at[i],
-            recv_sem=edge_recv.at[0],
+            dst_ref=fields.at[pl.ds(group * nb, 1)],
+            send_sem=in_edge_send.at[i],
+            recv_sem=in_edge_recv.at[0],
             device_id={"space": beyond + i},
             device_id_type=MESH,
         )
 
     total = jnp.zeros((8, LANES), f32)
-    copies = []
+    in_copies = []
     above_copy.wait_recv()
     below_copy.wait_recv()
     for c in [UNITS - 1] + list(range(UNITS - 1)):
@@ -303,59 +463,49 @@
             @pl.when(place == 0)
             def _():
                 for i in range(group):
-                    edge_copy(i).start()
+                    in_edge_copy(i).start()
 
         for i in reversed(range(1, group)):
             other = flip(place, i, group)
             copy = pltpu.make_async_remote_copy(
                 src_ref=mine.at[other, pl.ds(c * unit, unit)],
-                dst_ref=out.at[pl.ds(place * nb + c * unit, unit)],
-                send_sem=send_sem.at[c, i],
-                recv_sem=recv_sem.at[c, i],
+                dst_ref=fields.at[pl.ds(place * nb + c * unit, unit)],
+                send_sem=in_send_sem.at[c, i],
+                recv_sem=in_recv_sem.at[c, i],
                 device_id={"space": base + other},
                 device_id_type=MESH,
             )
             copy.start()
-            copies.append(copy)
-    theta[...] = total
+            in_copies.append(copy)
+    theta = total
 
     def keep(k, carry):
-        out[place * nb + k] = mine[place, k]
+        fields[place * nb + k] = mine[place, k]
         return carry
 
     lax.fori_loop(0, nb, keep, 0)
     for copy in rims + [below_copy, above_copy]:
         copy.wait_send()
-    for copy in copies:
+    for copy in in_copies:
         copy.wait()
-    edge_copy(0).wait_recv()
+    in_edge_copy(0).wait_recv()
 
     @pl.when(place == 0)
     def _():
         for i in range(group):
-            edge_copy(i).wait_send()
-
-
-def solve_kernel(
-    extent, group, fields, decay, weight, close, x_table, z_table, z_back, own_zero, far_zero,
-    smooth, one, two, modes, ends, far, mode, far_mode, outgo, held, edge_held,
-    end_send, end_recv, send_sem, recv_sem, edge_send, edge_recv,
-):
+            in_edge_copy(i).wait_send()
+
     n = extent
-    nb = smooth.shape[-1] // LANES
     planes = group * nb * LANES // (n * n)
     columns = n * n // LANES
     pairs = planes // 2
     lanes = planes * 4
     per = columns // PIECES
-    unit = nb // UNITS
-    me = lax.axis_index("space")
-    place = lax.rem(me, group)
-    base = me - place
-    beyond = group - base
     upper = lax.broadcasted_iota(jnp.int32, (8, LANES), 0) >= 4
-    barrier = greet([base + flip(place, i, group) for i in range(1, group)] + [beyond + i for i in range(group)])
-
+    x_table, z_table, z_back = (tables.at[i] for i in range(3))
+    decay, weight = wave.at[0], wave.at[1]
+    close = wave.at[pl.ds(2, 2)]
+    own_zero, far_zero = zero.at[0], zero.at[1]
     def rows_at(i):
         return pl.ds(pl.multiple_of(i * n, 8), n)
 
@@ -365,15 +515,13 @@
         full = jnp.concatenate(tiles + [jnp.zeros((rest, LANES), f32)], axis=0)
         one[block(c), :] = full.T
 
-    turn_in(0, [fields[planes * columns]])
-
     def turn_rest(c, carry):
         turn_in(c, [])
         return carry
 
-    lax.fori_loop(1, columns, turn_rest, 0)
+    lax.fori_loop(0, columns, turn_rest, 0, unroll=3)
+    turn_in(0, [fields[planes * columns]])
     one[0:n, :] = pltpu.roll(one[0:n, :], LANES - 4, 1)
-
     def along_x(i, carry):
         parts = [one[rows_at(2 * i + e), :] for e in range(2)]
         for e, v in enumerate(transform(x_table[...], parts)):
@@ -428,9 +576,8 @@
         lax.fori_loop(p * step_z, (p + 1) * step_z, along_z, 0, unroll=4)
         if p == 0:
             mode[...] = one[0:8, :]
-        lax.fori_loop(p * per, (p + 1) * per, reduce_ends, 0)
+        lax.fori_loop(p * per, (p + 1) * per, reduce_ends, 0, unroll=per)
         if p == 0:
-            pl.semaphore_wait(barrier, 2 * group - 1)
             mode_copy.start()
         end_copy(p).start()
 
@@ -473,7 +620,7 @@
         end_copy(p).wait_recv()
         if p == 0:
             mode_copy.wait_recv()
-        lax.fori_loop(p * per, (p + 1) * per, sweep, 0)
+        lax.fori_loop(p * per, (p + 1) * per, sweep, 0, unroll=per)
         if p == 0:
             exact = functools.partial(jnp.dot, preferred_element_type=f32, precision=lax.Precision.HIGHEST)
             flat = exact(mode[...], own_zero[...]) + exact(far_mode[...], far_zero[...])
@@ -486,9 +633,6 @@
         for e, v in enumerate(transform(x_table[...], parts)):
             one[rows_at(2 * i + e), :] = v
         return carry
-
-    lax.fori_loop(0, n // 2, back_x, 0, unroll=4)
-    one[0:n, :] = pltpu.roll(one[0:n, :], 4, 1)
 
     def turn_out(c):
         full = one[block(c), :].T
@@ -520,10 +664,12 @@
         device_id_type=MESH,
     )
 
-    full = turn_out(0)
-    outgo[planes * columns] = full[lanes : lanes + 4]
     for side in range(2):
-        lax.fori_loop(max(1, side * unit), (side + 1) * unit, turn_out_rest, 0)
+        lax.fori_loop(side * n // 4, (side + 1) * n // 4, back_x, 0, unroll=4)
+        if side == 0:
+            one[0:n, :] = pltpu.roll(one[0:n, :], 4, 1)
+            outgo[planes * columns] = turn_out(0)[lanes : lanes + 4]
+        lax.fori_loop(side * unit, (side + 1) * unit, turn_out_rest, 0, unroll=3)
         if side == 0:
             edge_copy.start()
         for i in reversed(range(1, group)):
@@ -542,179 +688,64 @@
     for p in range(PIECES):
         end_copy(p).wait_send()
     mode_copy.wait_send()
-    for i in reversed(range(1, group)):
-        for v in range(UNITS):
-            unit_copy(i, v).wait()
+    if True:
+        edge_copy.wait_send()
+
+    def edge_wait():
+        @pl.when(place == 0)
+        def _():
+            for i in range(group):
+                pltpu.make_async_remote_copy(
+                    src_ref=outgo.at[pl.ds(planes * columns, 1)],
+                    dst_ref=edge_held.at[i],
+                    send_sem=edge_send.at[0],
+                    recv_sem=edge_recv.at[i],
+                    device_id={"space": beyond},
+                    device_id_type=MESH,
+                ).wait_recv()
+            for a in range(8):
+                row = jnp.concatenate([edge_held[2 * a, 0], edge_held[2 * a + 1, 0]], axis=0)
+                smooth[a, :, 0:LANES] = jnp.where(lane_ids() < n, row, smooth[a, :, 0:LANES])
 
     def gather(k, carry):
         for a in range(8):
             smooth[a, :, block(k)] = jnp.concatenate([held[2 * a, k], held[2 * a + 1, k]], axis=0)
         return carry
 
-    lax.fori_loop(0, nb, gather, 0)
-    edge_copy.wait_send()
-
-    @pl.when(place == 0)
-    def _():
-        for i in range(group):
-            pltpu.make_async_remote_copy(
-                src_ref=outgo.at[pl.ds(planes * columns, 1)],
-                dst_ref=edge_held.at[i],
-                send_sem=edge_send.at[0],
-                recv_sem=edge_recv.at[i],
-                device_id={"space": beyond},
-                device_id_type=MESH,
-            ).wait_recv()
-        for a in range(8):
-            row = jnp.concatenate([edge_held[2 * a, 0], edge_held[2 * a + 1, 0]], axis=0)
-            smooth[a, :, 0:LANES] = jnp.where(lane_ids() < n, row, smooth[a, :, 0:LANES])
-
-
-def link_kernel(
-    extent, scales, links, smooth, theta, done, out_theta, out_deficit,
-    held, above, below, rot, mine, sums, load_sem, halo_send, halo_recv, send_sem, recv_sem,
-):
-    nb, slices = held.shape[0], held.shape[1]
-    n = sums.shape[0]
-    yb = extent * extent // LANES
-    unit = nb // UNITS
-    q = nb * LANES // extent
-    mid = (extent // 2) * extent
-    lane = lane_ids()
-    me = lax.axis_index("space")
-    ahead, behind = lax.rem(me + 1, n), lax.rem(me + n - 1, n)
-    loads = [fetch_block(links, held, load_sem, k) for k in range(nb)]
-    for copy in loads:
-        copy.start()
-    barrier = greet([lax.rem(me + i, n) for i in range(1, n)])
-
-    def rotate(values, sl):
-        g = rotation_of(values)
-        for i in range(3):
-            for j in range(3):
-                for p in range(2):
-                    rot[6 * i + 2 * j + p, :, sl] = g[i][j][p]
-
-    def rotate_own(k, carry):
-        rotate([smooth[a, :, block(k)] for a in range(8)], block(k))
-        return carry
-
-    def rotate_above(k, carry):
-        rotate([above[a, :, block(k)] for a in range(8)], block(nb + k))
-        return carry
-
-    def halo(i, source, dest, other):
-        return pltpu.make_async_remote_copy(
-            src_ref=source,
-            dst_ref=dest,
-            send_sem=halo_send.at[i],
-            recv_sem=halo_recv.at[i],
-            device_id={"space": other},
-            device_id_type=MESH,
-        )
-
-    def span(start, size):
-        return pl.ds(pl.multiple_of(start * LANES, LANES), size * LANES)
-
-    odd = lax.rem(me, 2)
-    pick = yb - odd * (yb - mid // LANES)
-    below_copy = halo(0, smooth.at[:, :, span(pick, 1)], below, ahead)
-    rims = [
-        halo(1 + i, smooth.at[:, :, span(i * unit, unit)], above.at[:, :, span(i * unit, unit)], behind)
-        for i in range(yb // unit)
-    ]
-
-    lax.fori_loop(0, unit, rotate_own, 0)
-    pl.semaphore_wait(barrier, n - 1)
-    for copy in [below_copy] + rims:
-        copy.start()
-    lax.fori_loop(unit, nb, rotate_own, 0)
-
-    def step(which, k, total):
-        sl = block(k)
-        before = block(jnp.maximum(k - 1, 0))
-        after = block(k + 1)
-        wrap = block(jnp.where(k == yb, 0, nb + yb))
-        x_at, row = site_of(k, extent)
-        edge_x = x_at == extent - 1
-        edge_z = at_z(row, extent - 1, me, q, extent)
-
-        def ahead_x(e):
-            cur = rot[e, :, sl]
-            near = pltpu.roll(jnp.where(lane == 0, rot[e, :, after], cur), LANES - 1, 1)
-            far = pltpu.roll(jnp.where(lane >= LANES - extent + 1, rot[e, :, before], cur), extent - 1, 1)
-            return jnp.where(edge_x, far, near)
-
-        def ahead_y(e):
-            return rot[e, :, block(k + yb)]
-
-        def ahead_z(e):
-            cur = rot[e, :, sl]
-            near = pltpu.roll(jnp.where(lane < extent, rot[e, :, after], cur), LANES - extent, 1)
-            far = pltpu.roll(rot[e, :, wrap], LANES - extent, 1)
-            return jnp.where(edge_z, far, near)
-
-        flat_out = flat_block(done, k)
-        for d in which:
-            forward = (ahead_x, ahead_y, ahead_z)[d]
-            u = load_link(flat_block(held, k), slices, d)
-            own = [[(rot[6 * i + 2 * j, :, sl], rot[6 * i + 2 * j + 1, :, sl]) for j in range(3)] for i in range(3)]
-            left = [
-                [dot_row(own[i], [u[k2][j] for k2 in range(3)], cmul) for j in range(3)]
-                for i in range(3)
-            ]
-            for j in range(3):
-                row3 = [(forward(6 * j + 2 * c), forward(6 * j + 2 * c + 1)) for c in range(3)]
-                for i in range(2):
-                    v = dot_row(left[i], row3, mul_conj)
-                    flat_out[rows_of(slices, d, i, j, 0), :] = v[0]
-                    flat_out[rows_of(slices, d, i, j, 1), :] = v[1]
-                    if i == j:
-                        total = total + (1.0 - v[0])
-                if j == 2:
-                    total = total + (1.0 - dot_row(left[2], row3, mul_conj)[0])
-        return total
-
-    for copy in loads:
-        copy.wait()
-    below_copy.wait_recv()
-    rotate([below[a] for a in range(8)], block(nb + yb))
-    total = jnp.zeros((8, LANES), f32)
-    total = lax.fori_loop(0, nb - yb, functools.partial(step, (0, 1, 2)), total)
-    total = lax.fori_loop(nb - yb, nb - 1, functools.partial(step, (0, 2)), total)
-    for i, copy in enumerate(rims):
-        copy.wait_recv()
-        lax.fori_loop(i * unit, (i + 1) * unit, rotate_above, 0)
-    total = lax.fori_loop(nb - yb, nb - 1, functools.partial(step, (1,)), total)
-    total = lax.fori_loop(nb - 1, nb, functools.partial(step, (0, 1, 2)), total)
+    def arrive(v):
+        for i in reversed(range(1, group)):
+            unit_copy(i, v).wait()
+        lax.fori_loop(v * unit, (v + 1) * unit, gather, 0)
+        if v == 0:
+            edge_wait()
+
+    total = link_part(extent, held_links, smooth, arrive, done, above, below, rot, late_send, late_recv, devices)
 
     wide_lane = lane_ids(slices)
-    t = jnp.sum(jnp.sum(theta[...], axis=1, keepdims=True), axis=0, keepdims=True)
+    t = jnp.sum(jnp.sum(theta, axis=1, keepdims=True), axis=0, keepdims=True)
     d = jnp.sum(total, axis=1, keepdims=True)
     own_row = lax.broadcasted_iota(jnp.int32, (slices, LANES), 0)
-    mine[...] = jnp.where(
+    spread = jnp.where(
         wide_lane == own_row, d, jnp.where(wide_lane == slices, jnp.where(own_row == 0, t, 0.0), 0.0)
     )
+    sum_row[...] = jnp.sum(spread, axis=0, keepdims=True)
     copies = []
-    for i in range(1, n):
+    for i in range(1, devices):
         copy = pltpu.make_async_remote_copy(
-            src_ref=mine,
+            src_ref=sum_row,
             dst_ref=sums.at[i],
-            send_sem=send_sem.at[i],
-            recv_sem=recv_sem.at[i],
-            device_id={"space": lax.rem(me + i, n)},
+            send_sem=sum_send.at[i],
+            recv_sem=sum_recv.at[i],
+            device_id={"space": lax.rem(me + i, devices)},
             device_id_type=MESH,
         )
         copy.start()
         copies.append(copy)
-    for copy in [below_copy] + rims:
-        copy.wait_send()
     for copy in copies:
         copy.wait()
-    total = mine[...]
-    for i in range(1, n):
-        total = total + sums[i]
-    row = jnp.sum(total, axis=0, keepdims=True)
+    row = sum_row[...]
+    for i in range(1, devices):
+        row = row + sums[i]
     out_deficit[...] = row[:, :slices] * scales[1]
     out_theta[...] = row[:, slices : slices + 1] * scales[0]
 
@@ -738,58 +769,21 @@
 
 
 ANY = pl.BlockSpec(memory_space=pl.ANY)
-
-
-def call(kernel, number, out_shape, scratch, *args, in_specs=None, out_specs=None, limit=60):
+HBM = pl.BlockSpec(memory_space=pltpu.HBM)
+
+
+def call(kernel, number, out_shape, scratch, *args, in_specs=None, out_specs=None, limit=0):
     return pl.pallas_call(
         kernel,
         out_shape=out_shape,
         in_specs=in_specs or [VM] * len(args),
         out_specs=out_specs or jax.tree.map(lambda _: VM, out_shape),
         scratch_shapes=scratch,
+        cost_estimate=pl.CostEstimate(flops=COST, bytes_accessed=COST // 1000, transcendentals=0),
         compiler_params=pltpu.CompilerParams(
-            collective_id=number, has_side_effects=True, vmem_limit_bytes=limit * 1024 * 1024
+            collective_id=number, has_side_effects=True, vmem_limit_bytes=limit * 1024
         ),
     )(*args)
-
-
-def wide(full):
-    full = full.astype(np.float32)
-    hi = full.astype(jnp.bfloat16)
-    lo = (full - hi.astype(np.float32)).astype(jnp.bfloat16)
-    return jnp.asarray(np.concatenate([hi, hi, lo], axis=1))
-
-
-def hartley(n, offset=0):
-    k = np.arange(n)
-    angle = 2.0 * np.pi / n * ((k[:, None] * (k[None, :] - offset)) % n)
-    return (np.cos(angle) + np.sin(angle)) / np.sqrt(n)
-
-
-def decay_tables(n, planes):
-    wave = 4.0 * np.sin(np.pi * np.arange(n) / n) ** 2
-    p = (wave[:, None] + wave[None, :]).reshape(-1)
-    p[0] = 1.0
-    mu = 1.0 + 0.5 * p - np.sqrt(p + 0.25 * p * p)
-    weight = top_momentum / (1.0 / mu - mu)
-    close = 1.0 / (1.0 - mu ** (2 * planes))
-    rows = np.stack([mu, weight, close, close * mu**planes])
-    rows[:, 0] = 0.0
-    rows = np.broadcast_to(rows[:, None, :], (4, 8, n * n)).astype(np.float32)
-    return jnp.asarray(rows[0]), jnp.asarray(rows[1]), jnp.asarray(rows[2:])
-
-
-def zero_tables(n, planes):
-    d = np.arange(n)
-    green = top_momentum * ((n * n - 1.0) / (12.0 * n) - d * (n - d) / (2.0 * n))
-    y = np.arange(planes)
-    outs = []
-    for shift in (0, planes):
-        small = green[(y[:, None] - y[None, :] + shift) % n]
-        full = np.zeros((LANES, LANES), np.float32)
-        full[: 4 * planes, : 4 * planes] = np.kron(small, np.eye(4))
-        outs.append(jnp.asarray(full))
-    return outs
 
 
 def body(links):
@@ -806,44 +800,27 @@
     assert group * 4 == 8 * slices and nb % UNITS == 0 and plane % (nb // UNITS * LANES) == 0
     rims = plane // (nb // UNITS * LANES)
     blocks = (nb, slices, 3, 2, 3, 2, LANES)
-    fields, theta = call(
-        functools.partial(spread_kernel, n, group),
+    times = lax.axis_size("tm")
+    scales = (1.0 / (slices * times * n**3), 1.0 / n**3)
+    placed, total, shares = call(
+        functools.partial(gauge_kernel, n, group, scales),
         1,
-        (shape(group * nb + 1, 4, LANES), shape(slices, LANES)),
+        (shape(*blocks), shape(1, 1), shape(1, slices)),
         [
-            *[vm(count, *blocks[1:]) for count in [1] + [nb // UNITS] * (UNITS - 1) + [nb // UNITS - 1]],
+            vm(*blocks), vm(8, slices, local), vm(8, slices, plane), vm(8, slices, LANES),
+            vm(18, slices, local + plane + LANES), vm(1, LANES), vm(devices, 1, LANES),
+            dma(rims + 1), dma(rims + 1), dma(devices), dma(devices),
             vm(3, 8, slices, local), vm(8, slices, plane), vm(8, slices, LANES), vm(8, slices, LANES),
-            vm(group, nb, 4, LANES), dma(nb), dma(rims + 2), dma(rims + 2),
+            vm(group, nb, 4, LANES), vm(group * nb + 1, 4, LANES), dma(nb), dma(rims + 2), dma(rims + 2),
             dma(UNITS, group), dma(UNITS, group), dma(group), dma(1),
-        ],
-        links,
-        in_specs=[ANY],
-    )
-    smooth = call(
-        functools.partial(solve_kernel, n, group),
-        2,
-        shape(8, slices, local),
-        [
+            vm(4, 8, plane), pltpu.VMEM((3, n, 3 * n), bf16), vm(2, LANES, LANES),
             vm(plane, LANES), vm(plane, LANES), vm(4 * planes, plane), vm(8, plane), vm(8, plane),
             vm(8, LANES), vm(8, LANES), vm(group * nb + 1, 4, LANES), vm(group, nb, 4, LANES), vm(group, 1, 4, LANES),
             dma(PIECES + 1), dma(PIECES + 1), dma(UNITS, group), dma(UNITS, group), dma(1), dma(group),
         ],
-        fields, *decay_tables(n, planes), wide(hartley(n)), wide(hartley(n, 1)), wide(hartley(n, 1).T), *zero_tables(n, planes),
-    )
-    times = lax.axis_size("tm")
-    scales = (1.0 / (slices * times * n**3), 1.0 / n**3)
-    placed, total, shares = call(
-        functools.partial(link_kernel, n, scales),
-        3,
-        (shape(*blocks), shape(1, 1), shape(1, slices)),
-        [
-            vm(*blocks), vm(8, slices, plane), vm(8, slices, LANES), vm(18, slices, local + plane + LANES),
-            vm(slices, LANES), vm(devices, slices, LANES), dma(nb), dma(rims + 1), dma(rims + 1),
-            dma(devices), dma(devices),
-        ],
-        links, smooth, theta,
-        in_specs=[ANY, VM, VM],
-        limit=LINK_MB,
+        links,
+        in_specs=[HBM],
+        limit=GAUGE_KB,
     )
     new_links = pl.pallas_call(
         place_kernel,

time: 84.9 us -> 72.4 us (0.85)
  Pallas kernels: 79.8 us -> 69.3 us
  local copies, waits for them, and re-layouts: 2.36 us -> 0.51 us
    pallas_call x3 -> x1, Pallas kernels: 77.7 us -> 67.2 us  [call(): pl.pallas_call(kernel, out_shape=out_shape, in_specs=in_specs or [VM] * l...]
    unnamed x7 -> x1, local copies, waits for them, and re-layouts: 2.36 us -> 0.51 us
where the time goes in v3:
time: 72.4 us; the launch traced here: 72.2 us
  Pallas kernels  69.3 us (96%)
  between operations  2.33 us (3%)
    pallas_call x1, Pallas kernels, call(): pl.pallas_call(kernel, out_shape=out_shape, in_specs=in_specs or [VM] * l...  67.2 us
    pallas_call x1, Pallas kernels, body(): pl.pallas_call(place_kernel, out_shape=shape(*links.shape), in_specs=[VM]...  2.16 us

profile of v3, /device:TPU:0, one launch (start us, length us, event | category | flops | bytes accessed | tf_op | source)
XLA Modules:
  0.0 72.2 jit_solution(2650953204372148768)
XLA Ops:
  0.6 67.2 %shard_map.38 = (f32[27,8,3,2,3,2,128]{6,5,4,3,2,1,0:T(2,128)S(1)}, f32[1,1]{1,0:T(1,128)}, f32[1,8]{1,0:T(1,128)S(1)}) custom-call(f32[8,3,2,3,2,3456]{5,4,3,2,1,0:T(2,128)} %links.1), custom_call_target="tpu_custom_call" | custom-call | flops 1000000000 | bytes 1000000 | tf_op jit(solution)/shard_map/pallas_call | solution.py:776
  67.8 2.2 %shard_map.39 = f32[8,3,2,3,2,3456]{5,4,3,2,1,0:T(2,128)} custom-call(f32[27,8,3,2,3,2,128]{6,5,4,3,2,1,0:T(2,128)S(1)} %get-tuple-element.6.blocks), custom_call_target="tpu_custom_call" | custom-call | tf_op jit(solution)/shard_map/pallas_call | solution.py:825
  70.5 0.5 copy.7

commit v4 on v3

--- a/solution.py
+++ b/solution.py
@@ -345,7 +345,7 @@
         held_links, smooth, above, below, rot, sum_row, sums, late_send, late_recv, sum_send, sum_recv,
         alg, y_rim, z_below, z_above, mine, fields, load_sem, halo_send, halo_recv,
         in_send_sem, in_recv_sem, in_edge_send, in_edge_recv,
-        wave, tables, zero, one, two, modes, ends, far, mode, far_mode, outgo, held, edge_held,
+        extra, extra_held, extra_send, extra_recv, tip_send, tip_recv, wave, tables, zero, one, two, modes, ends, far, mode, far_mode, outgo, held, edge_held,
         end_send, end_recv, send_sem, recv_sem, edge_send, edge_recv,
     ) = refs
     devices = 2 * group
@@ -369,6 +369,8 @@
 
     make_tables(extent, extent // 2, wave, tables, zero)
 
+    first = nb - yb
+
     def algebra(i):
         start, stop = in_spans[i]
 
@@ -377,6 +379,9 @@
             for d in range(3):
                 for a, v in enumerate(algebra_of(load_link(flat, slices, d))):
                     alg[d, a, :, block(k)] = v
+                    if d == 1 and start >= first:
+                        extra[2 * a, k - first] = v[:half]
+                        extra[2 * a + 1, k - first] = v[half:]
             return carry
 
         for copy in in_loads[i]:
@@ -396,7 +401,6 @@
     def span(start, size):
         return pl.ds(pl.multiple_of(start * LANES, LANES), size * LANES)
 
-    first = nb - yb
     rims = [
         halo(i, alg.at[1, :, :, span(first + i * unit, unit)], y_rim.at[:, :, span(i * unit, unit)], ahead)
         for i in range(yb // unit)
@@ -405,19 +409,78 @@
     odd = lax.rem(me, 2)
     above_copy = halo(len(rims) + 1, alg.at[2, :, :, span(odd * (mid // LANES), 1)], z_above, behind)
 
+    last = lax.div(place + 1, group)
+    next_base = base + last * (beyond - base)
+    slot = lax.div(lax.rem(place + 1, group), 2)
+
+    def extra_copy(u, i):
+        other = flip(place, i, group)
+        return pltpu.make_async_remote_copy(
+            src_ref=extra.at[other, pl.ds(u * unit, unit)],
+            dst_ref=extra_held.at[pl.ds(slot * yb + u * unit, unit)],
+            send_sem=extra_send.at[u, i],
+            recv_sem=extra_recv.at[u, slot],
+            device_id={"space": next_base + other},
+            device_id_type=MESH,
+        )
+
+    def tip_copy(i):
+        other = flip(place, i, group)
+        return pltpu.make_async_remote_copy(
+            src_ref=extra.at[other, pl.ds(0, 1)],
+            dst_ref=extra_held.at[pl.ds(group // 2 * yb, 1)],
+            send_sem=tip_send.at[i],
+            recv_sem=tip_recv.at[0],
+            device_id={"space": base + other},
+            device_id_type=MESH,
+        )
+
+    def send_rim(u):
+        @pl.when(odd == 0)
+        def _():
+            rims[u].start()
+
+        @pl.when(odd == 1)
+        def _():
+            for i in reversed(range(1, group)):
+                extra_copy(u, i).start()
+
+        @pl.when(last == 1)
+        def _():
+            extra_copy(u, 0).start()
+
     algebra(0)
     algebra(1)
     pl.semaphore_wait(barrier, devices - 1)
     above_copy.start()
-    rims[0].start()
+    send_rim(0)
     for i in range(1, len(rims)):
         algebra(1 + i)
         if i == len(rims) - 1:
             below_copy.start()
-        rims[i].start()
+        send_rim(i)
+
+    @pl.when(last == 1)
+    def _():
+        for i in range(1, group):
+            tip_copy(i).start()
+        extra_held[group // 2 * yb] = extra[place, 0]
+
+    @pl.when(odd == 0)
+    def _():
+        y_rim[...] = jnp.zeros_like(y_rim)
+
     algebra(UNITS)
 
-    def step(from_rim, k, total):
+    @pl.when((odd == 1) & (last == 0))
+    def _():
+        def keep_extra(k, carry):
+            extra_held[slot * yb + k] = extra[place, k]
+            return carry
+
+        lax.fori_loop(0, yb, keep_extra, 0)
+
+    def step(from_rim, k, carry):
         sl = block(k)
         before = block(jnp.maximum(k - 1, 0))
         after = block(jnp.minimum(k + 1, nb - 1))
@@ -435,10 +498,9 @@
             far = pltpu.roll(jnp.where(k == 0, alg[2, a, :, block(yb)], z_above[a]), extent, 1)
             bz = jnp.where(edge_z, far, near)
             b = (bx - x) + (by - y) + (bz - z)
-            total = total + b * b
             mine[2 * a, k] = b[:half]
             mine[2 * a + 1, k] = b[half:]
-        return total
+        return carry
 
     def in_edge_copy(i):
         return pltpu.make_async_remote_copy(
@@ -450,14 +512,17 @@
             device_id_type=MESH,
         )
 
-    total = jnp.zeros((8, LANES), f32)
     in_copies = []
     above_copy.wait_recv()
     below_copy.wait_recv()
     for c in [UNITS - 1] + list(range(UNITS - 1)):
         if c < len(rims):
-            rims[c].wait_recv()
-        total = lax.fori_loop(c * unit, (c + 1) * unit, functools.partial(step, c < len(rims)), total)
+
+            @pl.when(odd == 1)
+            def _():
+                rims[c].wait_recv()
+
+        lax.fori_loop(c * unit, (c + 1) * unit, functools.partial(step, c < len(rims)), 0)
         if c == 0:
 
             @pl.when(place == 0)
@@ -477,18 +542,55 @@
             )
             copy.start()
             in_copies.append(copy)
-    theta = total
-
     def keep(k, carry):
         fields[place * nb + k] = mine[place, k]
         return carry
 
     lax.fori_loop(0, nb, keep, 0)
-    for copy in rims + [below_copy, above_copy]:
+    for copy in [below_copy, above_copy]:
         copy.wait_send()
+
+    @pl.when(odd == 0)
+    def _():
+        for copy in rims:
+            copy.wait_send()
+
+    @pl.when(odd == 1)
+    def _():
+        for u in range(len(rims)):
+            for i in range(1, group):
+                extra_copy(u, i).wait_send()
+
+    @pl.when(last == 1)
+    def _():
+        for u in range(len(rims)):
+            extra_copy(u, 0).wait_send()
+        for i in range(1, group):
+            tip_copy(i).wait_send()
+
     for copy in in_copies:
         copy.wait()
     in_edge_copy(0).wait_recv()
+
+    @pl.when(last == 0)
+    def _():
+        tip_copy(1).wait_recv()
+
+    def wait_extra(m):
+        @pl.when(place != 2 * m - 1)
+        def _():
+            for u in range(len(rims)):
+                pltpu.make_async_remote_copy(
+                    src_ref=extra.at[0, pl.ds(u * unit, unit)],
+                    dst_ref=extra_held.at[pl.ds(m * yb + u * unit, unit)],
+                    send_sem=extra_send.at[u, 0],
+                    recv_sem=extra_recv.at[u, m],
+                    device_id={"space": beyond},
+                    device_id_type=MESH,
+                ).wait_recv()
+
+    for m in range(group // 2):
+        wait_extra(m)
 
     @pl.when(place == 0)
     def _():
@@ -509,18 +611,23 @@
     def rows_at(i):
         return pl.ds(pl.multiple_of(i * n, 8), n)
 
-    def turn_in(c, extra):
-        tiles = [fields[y * columns + c] for y in range(planes)] + extra
+    def turn_in(c, tip):
+        tiles = [fields[y * columns + c] for y in range(planes)]
+        for m in range(group // 2):
+            y = m * (planes // (group // 2))
+            tiles[y] = tiles[y] + extra_held[m * yb + c]
+        tiles = tiles + tip
         rest = LANES - 4 * len(tiles)
         full = jnp.concatenate(tiles + [jnp.zeros((rest, LANES), f32)], axis=0)
         one[block(c), :] = full.T
-
-    def turn_rest(c, carry):
-        turn_in(c, [])
-        return carry
-
-    lax.fori_loop(0, columns, turn_rest, 0, unroll=3)
-    turn_in(0, [fields[planes * columns]])
+        return full
+
+    def turn_rest(c, total):
+        full = turn_in(c, [])
+        return total + sum(full[8 * i : 8 * i + 8] * full[8 * i : 8 * i + 8] for i in range(lanes // 8))
+
+    theta = lax.fori_loop(0, columns, turn_rest, jnp.zeros((8, LANES), f32), unroll=3)
+    turn_in(0, [fields[planes * columns] + extra_held[group // 2 * yb]])
     one[0:n, :] = pltpu.roll(one[0:n, :], LANES - 4, 1)
     def along_x(i, carry):
         parts = [one[rows_at(2 * i + e), :] for e in range(2)]
@@ -688,8 +795,7 @@
     for p in range(PIECES):
         end_copy(p).wait_send()
     mode_copy.wait_send()
-    if True:
-        edge_copy.wait_send()
+    edge_copy.wait_send()
 
     def edge_wait():
         @pl.when(place == 0)
@@ -813,6 +919,8 @@
             vm(3, 8, slices, local), vm(8, slices, plane), vm(8, slices, LANES), vm(8, slices, LANES),
             vm(group, nb, 4, LANES), vm(group * nb + 1, 4, LANES), dma(nb), dma(rims + 2), dma(rims + 2),
             dma(UNITS, group), dma(UNITS, group), dma(group), dma(1),
+            vm(group, plane // LANES, 4, LANES), vm(devices // 4 * (plane // LANES) + 1, 4, LANES),
+            dma(rims, group), dma(rims, group // 2), dma(group), dma(1),
             vm(4, 8, plane), pltpu.VMEM((3, n, 3 * n), bf16), vm(2, LANES, LANES),
             vm(plane, LANES), vm(plane, LANES), vm(4 * planes, plane), vm(8, plane), vm(8, plane),
             vm(8, LANES), vm(8, LANES), vm(group * nb + 1, 4, LANES), vm(group, nb, 4, LANES), vm(group, 1, 4, LANES),

time: 72.4 us -> 70.3 us (0.971)
  Pallas kernels: 69.3 us -> 67.3 us
    pallas_call x1, Pallas kernels: 67.2 us -> 65.1 us  [call(): pl.pallas_call(kernel, out_shape=out_shape, in_specs=in_specs or [VM] * l...]
where the time goes in v4:
time: 70.3 us; the launch traced here: 70.1 us
  Pallas kernels  67.3 us (96%)
  between operations  2.33 us (3%)
    pallas_call x1, Pallas kernels, call(): pl.pallas_call(kernel, out_shape=out_shape, in_specs=in_specs or [VM] * l...  65.1 us
    pallas_call x1, Pallas kernels, body(): pl.pallas_call(place_kernel, out_shape=shape(*links.shape), in_specs=[VM]...  2.16 us

profile of v4, /device:TPU:0, one launch (start us, length us, event | category | flops | bytes accessed | tf_op | source)
XLA Modules:
  0.0 70.1 jit_solution(12300482423528629143)
XLA Ops:
  0.6 65.1 %shard_map.38 = (f32[27,8,3,2,3,2,128]{6,5,4,3,2,1,0:T(2,128)S(1)}, f32[1,1]{1,0:T(1,128)}, f32[1,8]{1,0:T(1,128)S(1)}) custom-call(f32[8,3,2,3,2,3456]{5,4,3,2,1,0:T(2,128)} %links.1), custom_call_target="tpu_custom_call" | custom-call | flops 1000000000 | bytes 1000000 | tf_op jit(solution)/shard_map/pallas_call | solution.py:882
  65.7 2.2 %shard_map.39 = f32[8,3,2,3,2,3456]{5,4,3,2,1,0:T(2,128)} custom-call(f32[27,8,3,2,3,2,128]{6,5,4,3,2,1,0:T(2,128)S(1)} %get-tuple-element.6.blocks), custom_call_target="tpu_custom_call" | custom-call | tf_op jit(solution)/shard_map/pallas_call | solution.py:933
  68.5 0.5 copy.7

commit v5 on v4

--- a/solution.py
+++ b/solution.py
@@ -222,7 +222,7 @@
         zero[i] = jnp.where(used, green, 0.0)
 
 
-def link_part(extent, held, smooth, arrive, done, above, below, rot, halo_send, halo_recv, n):
+def link_part(extent, held, smooth, arrive, mend_edges, done, below, rot, halo_send, halo_recv, n):
     nb, slices = held.shape[0], held.shape[1]
     yb = extent * extent // LANES
     unit = nb // UNITS
@@ -242,10 +242,6 @@
         rotate([smooth[a, :, block(k)] for a in range(8)], block(k))
         return carry
 
-    def rotate_above(k, carry):
-        rotate([above[a, :, block(k)] for a in range(8)], block(nb + k))
-        return carry
-
     def halo(i, source, dest, other):
         return pltpu.make_async_remote_copy(
             src_ref=source,
@@ -263,16 +259,12 @@
     pick = yb - odd * (yb - mid // LANES)
     below_copy = halo(0, smooth.at[:, :, span(pick, 1)], below, ahead)
     rims = [
-        halo(1 + i, smooth.at[:, :, span(i * unit, unit)], above.at[:, :, span(i * unit, unit)], behind)
-        for i in range(yb // unit)
+        halo(1 + i, smooth.at[:, :, span(i * unit, unit)], smooth.at[:, :, span(nb + i * unit, unit)], behind)
+        for i in range(2)
     ]
 
-    for v in range(UNITS):
-        arrive(v)
+    def turn(v):
         lax.fori_loop(v * unit, (v + 1) * unit, rotate_own, 0)
-        if v < len(rims):
-            rims[v].start()
-    below_copy.start()
 
     def step(which, k, total):
         sl = block(k)
@@ -321,20 +313,51 @@
             total = total + ((1.0 - p00[0]) + (1.0 - p11[0]) + (1.0 - minor))
         return total
 
-    total = jnp.zeros((8, LANES), f32)
-    total = lax.fori_loop(1, nb - yb, functools.partial(step, (0, 1, 2)), total)
+    def links_of(start, stop, dirs, total):
+        return lax.fori_loop(start, stop, functools.partial(step, dirs), total)
+
+    arrive(odd)
+    arrive(odd + 2)
+    mend_edges()
+    turn(odd)
+    turn(odd + 2)
+
+    @pl.when(odd == 1)
+    def _():
+        rims[1].start()
+
+    below_copy.start()
+    total = links_of(odd * unit, (odd + 1) * unit, (1,), jnp.zeros((8, LANES), f32))
+    arrive(1 - odd)
+    turn(1 - odd)
+
+    @pl.when(odd == 1)
+    def _():
+        rims[0].start()
+        for v in (2, 4):
+            arrive(jnp.int32(v))
+            turn(v)
+
     below_copy.wait_recv()
     rotate([below[a] for a in range(8)], block(nb + yb))
-    total = lax.fori_loop(0, 1, functools.partial(step, (0, 1, 2)), total)
-    total = lax.fori_loop(nb - yb, nb - 1, functools.partial(step, (0, 2)), total)
-    for i, copy in enumerate(rims):
-        copy.wait_recv()
-        lax.fori_loop(i * unit, (i + 1) * unit, rotate_above, 0)
-        last = i == len(rims) - 1
-        total = lax.fori_loop(nb - yb + i * unit, nb - yb + (i + 1) * unit - last, functools.partial(step, (1,)), total)
-    total = lax.fori_loop(nb - 1, nb, functools.partial(step, (0, 1, 2)), total)
-    for copy in [below_copy] + rims:
-        copy.wait_send()
+    total = links_of(0, nb - 1, (0, 2), total)
+
+    @pl.when(odd == 0)
+    def _():
+        for v in (3, 4):
+            rims[v - 3].wait_recv()
+            turn(v)
+
+    total = links_of((1 - odd) * unit, (2 - odd) * unit, (1,), total)
+    total = links_of(2 * unit, nb - 1, (1,), total)
+    total = links_of(nb - 1, nb, (0, 1, 2), total)
+    below_copy.wait_send()
+
+    @pl.when(odd == 1)
+    def _():
+        for copy in rims:
+            copy.wait_send()
+
     return total
 
 
@@ -342,7 +365,7 @@
     extent, group, scales, links, done, out_theta, out_deficit, *refs
 ):
     (
-        held_links, smooth, above, below, rot, sum_row, sums, late_send, late_recv, sum_send, sum_recv,
+        held_links, smooth, below, rot, sum_row, sums, late_send, late_recv, sum_send, sum_recv,
         alg, y_rim, z_below, z_above, mine, fields, load_sem, halo_send, halo_recv,
         in_send_sem, in_recv_sem, in_edge_send, in_edge_recv,
         extra, extra_held, extra_send, extra_recv, tip_send, tip_recv, wave, tables, zero, one, two, modes, ends, far, mode, far_mode, outgo, held, edge_held,
@@ -753,23 +776,45 @@
 
     def unit_copy(i, v):
         other = flip(place, i, group)
+        wrap = lax.div(v, UNITS) * lax.div(other + 1, group)
         return pltpu.make_async_remote_copy(
-            src_ref=outgo.at[pl.ds(other * nb + v * unit, unit)],
+            src_ref=outgo.at[pl.ds(other * nb + v * unit - wrap * (planes * columns), unit)],
             dst_ref=held.at[place, pl.ds(v * unit, unit)],
             send_sem=send_sem.at[v, i],
             recv_sem=recv_sem.at[v, i],
-            device_id={"space": base + other},
+            device_id={"space": base + other + wrap * (beyond - base)},
             device_id_type=MESH,
         )
 
-    edge_copy = pltpu.make_async_remote_copy(
-        src_ref=outgo.at[pl.ds(planes * columns, 1)],
-        dst_ref=edge_held.at[place],
-        send_sem=edge_send.at[0],
-        recv_sem=edge_recv.at[place],
-        device_id={"space": beyond},
-        device_id_type=MESH,
-    )
+    def edge_copy(i, other):
+        return pltpu.make_async_remote_copy(
+            src_ref=outgo.at[pl.ds(planes * columns, 1)],
+            dst_ref=edge_held.at[place],
+            send_sem=edge_send.at[i],
+            recv_sem=edge_recv.at[place],
+            device_id={"space": other},
+            device_id_type=MESH,
+        )
+
+    edges = [edge_copy(0, beyond), edge_copy(1, base + group - 1)]
+
+    def each_unit(side, act):
+        for i in reversed(range(1, group)):
+            parity = lax.rem(place + i, 2)
+            if side == 0:
+                act(unit_copy(i, parity))
+                act(unit_copy(i, parity + 2))
+            else:
+                act(unit_copy(i, 1 - parity))
+
+                @pl.when(parity == 1)
+                def _():
+                    act(unit_copy(i, jnp.int32(2)))
+                    act(unit_copy(i, jnp.int32(4)))
+
+        @pl.when(last == 1)
+        def _():
+            act(unit_copy(0, jnp.int32(3 + side)))
 
     for side in range(2):
         lax.fori_loop(side * n // 4, (side + 1) * n // 4, back_x, 0, unroll=4)
@@ -778,54 +823,86 @@
             outgo[planes * columns] = turn_out(0)[lanes : lanes + 4]
         lax.fori_loop(side * unit, (side + 1) * unit, turn_out_rest, 0, unroll=3)
         if side == 0:
-            edge_copy.start()
-        for i in reversed(range(1, group)):
-            odd = lax.rem(place + i + side, 2)
-            unit_copy(i, odd).start()
-
-            @pl.when(odd == 0)
+            edges[0].start()
+
+            @pl.when(last == 0)
             def _():
-                unit_copy(i, 2).start()
+                edges[1].start()
+
+        each_unit(side, lambda copy: copy.start())
 
     def keep(k, carry):
         held[place, k] = outgo[place * nb + k]
         return carry
 
     lax.fori_loop(0, nb, keep, 0)
+
+    @pl.when((odd == 1) & (last == 0))
+    def _():
+        lax.fori_loop(nb, nb + yb, keep, 0)
+
+    @pl.when(last == 1)
+    def _():
+        edge_held[place] = outgo[planes * columns : planes * columns + 1]
+
+    def edge_wait(i):
+        pltpu.make_async_remote_copy(
+            src_ref=outgo.at[pl.ds(planes * columns, 1)],
+            dst_ref=edge_held.at[i],
+            send_sem=edge_send.at[0],
+            recv_sem=edge_recv.at[i],
+            device_id={"space": beyond},
+            device_id_type=MESH,
+        ).wait_recv()
+
+    def mend(start):
+        for a in range(8):
+            row = jnp.concatenate([edge_held[2 * a, 0], edge_held[2 * a + 1, 0]], axis=0)
+            smooth[a, :, start : start + LANES] = jnp.where(
+                lane_ids() < n, row, smooth[a, :, start : start + LANES]
+            )
+
+    def gather(k, carry):
+        for a in range(8):
+            smooth[a, :, block(k)] = jnp.concatenate([held[2 * a, k], held[2 * a + 1, k]], axis=0)
+        return carry
+
+    def arrive(v):
+        for i in reversed(range(1, group)):
+            unit_copy(i, v).wait_recv()
+
+        @pl.when(last * lax.div(v, UNITS) == 1)
+        def _():
+            unit_copy(0, v).wait_recv()
+
+        lax.fori_loop(v * unit, (v + 1) * unit, gather, 0)
+
+    def mend_edges():
+        @pl.when(place == 0)
+        def _():
+            for i in range(group):
+                edge_wait(i)
+            mend(0)
+
+        @pl.when(last == 1)
+        def _():
+            for i in range(group - 1):
+                edge_wait(i)
+            mend(nb * LANES)
+
+    total = link_part(extent, held_links, smooth, arrive, mend_edges, done, below, rot, late_send, late_recv, devices)
     for p in range(PIECES):
         end_copy(p).wait_send()
     mode_copy.wait_send()
-    edge_copy.wait_send()
-
-    def edge_wait():
-        @pl.when(place == 0)
-        def _():
-            for i in range(group):
-                pltpu.make_async_remote_copy(
-                    src_ref=outgo.at[pl.ds(planes * columns, 1)],
-                    dst_ref=edge_held.at[i],
-                    send_sem=edge_send.at[0],
-                    recv_sem=edge_recv.at[i],
-                    device_id={"space": beyond},
-                    device_id_type=MESH,
-                ).wait_recv()
-            for a in range(8):
-                row = jnp.concatenate([edge_held[2 * a, 0], edge_held[2 * a + 1, 0]], axis=0)
-                smooth[a, :, 0:LANES] = jnp.where(lane_ids() < n, row, smooth[a, :, 0:LANES])
-
-    def gather(k, carry):
-        for a in range(8):
-            smooth[a, :, block(k)] = jnp.concatenate([held[2 * a, k], held[2 * a + 1, k]], axis=0)
-        return carry
-
-    def arrive(v):
-        for i in reversed(range(1, group)):
-            unit_copy(i, v).wait()
-        lax.fori_loop(v * unit, (v + 1) * unit, gather, 0)
-        if v == 0:
-            edge_wait()
-
-    total = link_part(extent, held_links, smooth, arrive, done, above, below, rot, late_send, late_recv, devices)
+    edges[0].wait_send()
+
+    @pl.when(last == 0)
+    def _():
+        edges[1].wait_send()
+
+    for side in range(2):
+        each_unit(side, lambda copy: copy.wait_send())
+
 
     wide_lane = lane_ids(slices)
     t = jnp.sum(jnp.sum(theta, axis=1, keepdims=True), axis=0, keepdims=True)
@@ -856,13 +933,20 @@
     out_theta[...] = row[:, slices : slices + 1] * scales[0]
 
 
-def place_kernel(blocks, out, sem):
+def place_kernel(blocks, theta, deficit, out, out_theta, out_deficit, held_theta, held_deficit, small, sem):
     copies = [
         pltpu.make_async_copy(blocks.at[k], out.at[:, :, :, :, :, pl.ds(k * LANES, LANES)], sem.at[k])
         for k in range(blocks.shape[0])
     ]
     for copy in copies:
         copy.start()
+    moves = [[(theta, held_theta), (held_theta, out_theta)], [(deficit, held_deficit), (held_deficit, out_deficit)]]
+    for leg in range(2):
+        short = [pltpu.make_async_copy(*move[leg], small.at[i]) for i, move in enumerate(moves)]
+        for copy in short:
+            copy.start()
+        for copy in short:
+            copy.wait()
     for copy in copies:
         copy.wait()
 
@@ -913,9 +997,9 @@
         1,
         (shape(*blocks), shape(1, 1), shape(1, slices)),
         [
-            vm(*blocks), vm(8, slices, local), vm(8, slices, plane), vm(8, slices, LANES),
+            vm(*blocks), vm(8, slices, local + plane), vm(8, slices, LANES),
             vm(18, slices, local + plane + LANES), vm(1, LANES), vm(devices, 1, LANES),
-            dma(rims + 1), dma(rims + 1), dma(devices), dma(devices),
+            dma(3), dma(3), dma(devices), dma(devices),
             vm(3, 8, slices, local), vm(8, slices, plane), vm(8, slices, LANES), vm(8, slices, LANES),
             vm(group, nb, 4, LANES), vm(group * nb + 1, 4, LANES), dma(nb), dma(rims + 2), dma(rims + 2),
             dma(UNITS, group), dma(UNITS, group), dma(group), dma(1),
@@ -923,21 +1007,21 @@
             dma(rims, group), dma(rims, group // 2), dma(group), dma(1),
             vm(4, 8, plane), pltpu.VMEM((3, n, 3 * n), bf16), vm(2, LANES, LANES),
             vm(plane, LANES), vm(plane, LANES), vm(4 * planes, plane), vm(8, plane), vm(8, plane),
-            vm(8, LANES), vm(8, LANES), vm(group * nb + 1, 4, LANES), vm(group, nb, 4, LANES), vm(group, 1, 4, LANES),
-            dma(PIECES + 1), dma(PIECES + 1), dma(UNITS, group), dma(UNITS, group), dma(1), dma(group),
+            vm(8, LANES), vm(8, LANES), vm(group * nb + 1, 4, LANES), vm(group, nb + plane // LANES, 4, LANES), vm(group, 1, 4, LANES),
+            dma(PIECES + 1), dma(PIECES + 1), dma(UNITS + rims, group), dma(UNITS + rims, group), dma(2), dma(group),
         ],
         links,
         in_specs=[HBM],
         limit=GAUGE_KB,
     )
-    new_links = pl.pallas_call(
+    new_links, total, shares = pl.pallas_call(
         place_kernel,
-        out_shape=shape(*links.shape),
-        in_specs=[VM],
-        out_specs=ANY,
-        scratch_shapes=[dma(nb)],
+        out_shape=(shape(*links.shape), shape(1, 1), shape(1, slices)),
+        in_specs=[VM, ANY, ANY],
+        out_specs=(ANY, ANY, ANY),
+        scratch_shapes=[vm(1, 1), vm(1, slices), dma(2), dma(nb)],
         compiler_params=pltpu.CompilerParams(vmem_limit_bytes=8 * 1024 * 1024),
-    )(placed)
+    )(placed, total, shares)
     total = total.reshape(())
     if times > 1:
         total = lax.psum(total, "tm")

time: 70.3 us -> 67.2 us (0.956)
  between operations: 2.33 us -> 0.64 us
  Pallas kernels: 67.3 us -> 66.4 us
    pallas_call x1, Pallas kernels: 65.1 us -> 63.6 us  [call(): pl.pallas_call(kernel, out_shape=out_shape, in_specs=in_specs or [VM] * l...]
where the time goes in v5:
time: 67.2 us; the launch traced here: 67 us
  Pallas kernels  66.4 us (99%)
    pallas_call x1, Pallas kernels, call(): pl.pallas_call(kernel, out_shape=out_shape, in_specs=in_specs or [VM] * l...  63.6 us
    pallas_call x1, Pallas kernels, body(): pl.pallas_call(place_kernel, out_shape=(shape(*links.shape), shape(1, 1),...  2.81 us

profile of v5, /device:TPU:0, one launch (start us, length us, event | category | flops | bytes accessed | tf_op | source)
XLA Modules:
  0.0 67.0 jit_solution(14527009739089982916)
XLA Ops:
  0.6 63.6 %shard_map.38 = (f32[27,8,3,2,3,2,128]{6,5,4,3,2,1,0:T(2,128)S(1)}, f32[1,1]{1,0:T(1,128)}, f32[1,8]{1,0:T(1,128)S(1)}) custom-call(f32[8,3,2,3,2,3456]{5,4,3,2,1,0:T(2,128)} %links.1), custom_call_target="tpu_custom_call" | custom-call | flops 1000000000 | bytes 1000000 | tf_op jit(solution)/shard_map/pallas_call | solution.py:966
  64.2 2.8 %shard_map.39 = (f32[8,3,2,3,2,3456]{5,4,3,2,1,0:T(2,128)}, f32[1,1]{1,0:T(1,128)}, f32[1,8]{1,0:T(1,128)}) custom-call(f32[27,8,3,2,3,2,128]{6,5,4,3,2,1,0:T(2,128)S(1)} %get-tuple-element.9.blocks, f32[1,1]{1,0:T(1,128)} %get-tuple-element.10.theta, f32[1,8]{1,0:T(1,128)S(1)} %get-tuple-element.11.deficit), custom_call_target="tpu_custom_call" | custom-call | tf_op jit(solution)/shard_map/pallas_call | solution.py:1017

commit v6 on v5

--- a/solution.py
+++ b/solution.py
@@ -189,6 +189,18 @@
 def divide(v, n):
     whole = jnp.floor((v + 0.5) * (1.0 / n))
     return whole, v - n * whole
+
+
+def send_order(group):
+    axes = group.bit_length() - 2
+    hops = lambda i: bin(i >> 1).count("1")
+    near = sorted((i for i in range(2, group) if hops(i) == 1), key=lambda i: (i & 1, -i))
+    far = sorted((i for i in range(2, group) if hops(i) > 1), key=lambda i: (-hops(i), -i))
+    order = []
+    while near:
+        order += far[:1] + near[:axes]
+        far, near = far[1:], near[axes:]
+    return order + far + [1]
 
 
 def make_tables(n, planes, wave, tables, zero):
@@ -327,7 +339,11 @@
         rims[1].start()
 
     below_copy.start()
-    total = links_of(odd * unit, (odd + 1) * unit, (1,), jnp.zeros((8, LANES), f32))
+    start = odd * unit
+    total = links_of(start, start + 1, (1,), jnp.zeros((8, LANES), f32))
+    total = links_of(start + 1, start + unit - 1, (0, 1, 2), total)
+    total = links_of(start + unit - 1, start + unit, (1,), total)
+    total = links_of(2 * unit + 1, 2 * unit + 1 + (1 - odd) * (unit - 2), (0, 2), total)
     arrive(1 - odd)
     turn(1 - odd)
 
@@ -340,7 +356,8 @@
 
     below_copy.wait_recv()
     rotate([below[a] for a in range(8)], block(nb + yb))
-    total = links_of(0, nb - 1, (0, 2), total)
+    total = links_of(0, start + 1, (0, 2), total)
+    total = links_of(start + unit - 1, 2 * unit + 1 + odd * (unit - 2), (0, 2), total)
 
     @pl.when(odd == 0)
     def _():
@@ -390,8 +407,6 @@
         copy.start()
     barrier = greet([base + flip(place, i, group) for i in range(1, group)] + [beyond + i for i in range(group)])
 
-    make_tables(extent, extent // 2, wave, tables, zero)
-
     first = nb - yb
 
     def algebra(i):
@@ -465,7 +480,7 @@
 
         @pl.when(odd == 1)
         def _():
-            for i in reversed(range(1, group)):
+            for i in send_order(group):
                 extra_copy(u, i).start()
 
         @pl.when(last == 1)
@@ -503,7 +518,7 @@
 
         lax.fori_loop(0, yb, keep_extra, 0)
 
-    def step(from_rim, k, carry):
+    def step(k, carry):
         sl = block(k)
         before = block(jnp.maximum(k - 1, 0))
         after = block(jnp.minimum(k + 1, nb - 1))
@@ -515,7 +530,11 @@
             near = pltpu.roll(jnp.where(lane == LANES - 1, alg[0, a, :, before], x), 1, 1)
             far = pltpu.roll(jnp.where(lane < extent - 1, alg[0, a, :, after], x), LANES - extent + 1, 1)
             bx = jnp.where(edge_x, far, near)
-            by = y_rim[a, :, sl] if from_rim else alg[1, a, :, block(k - yb)]
+            by = jnp.where(
+                k < yb,
+                y_rim[a, :, block(jnp.minimum(k, yb - 1))],
+                alg[1, a, :, block(jnp.maximum(k - yb, 0))],
+            )
             prev = jnp.where(k == 0, z_below[a], alg[2, a, :, before])
             near = pltpu.roll(jnp.where(lane >= LANES - extent, prev, z), extent, 1)
             far = pltpu.roll(jnp.where(k == 0, alg[2, a, :, block(yb)], z_above[a]), extent, 1)
@@ -535,36 +554,38 @@
             device_id_type=MESH,
         )
 
-    in_copies = []
     above_copy.wait_recv()
     below_copy.wait_recv()
-    for c in [UNITS - 1] + list(range(UNITS - 1)):
-        if c < len(rims):
-
-            @pl.when(odd == 1)
-            def _():
-                rims[c].wait_recv()
-
-        lax.fori_loop(c * unit, (c + 1) * unit, functools.partial(step, c < len(rims)), 0)
-        if c == 0:
+
+    @pl.when(odd == 1)
+    def _():
+        for copy in rims:
+            copy.wait_recv()
+
+    def in_copy(u, i):
+        other = flip(place, i, group)
+        return pltpu.make_async_remote_copy(
+            src_ref=mine.at[other, pl.ds(u * unit, unit)],
+            dst_ref=fields.at[pl.ds(place * nb + u * unit, unit)],
+            send_sem=in_send_sem.at[u, i],
+            recv_sem=in_recv_sem.at[u, i],
+            device_id={"space": base + other},
+            device_id_type=MESH,
+        )
+
+    for c, u in enumerate([2 - odd, 2 * odd, 1 - odd]):
+        lax.fori_loop(u * unit, (u + 1) * unit, step, 0)
+        for i in send_order(group):
+            in_copy(u, i).start()
+        if c == 1:
 
             @pl.when(place == 0)
             def _():
                 for i in range(group):
                     in_edge_copy(i).start()
 
-        for i in reversed(range(1, group)):
-            other = flip(place, i, group)
-            copy = pltpu.make_async_remote_copy(
-                src_ref=mine.at[other, pl.ds(c * unit, unit)],
-                dst_ref=fields.at[pl.ds(place * nb + c * unit, unit)],
-                send_sem=in_send_sem.at[c, i],
-                recv_sem=in_recv_sem.at[c, i],
-                device_id={"space": base + other},
-                device_id_type=MESH,
-            )
-            copy.start()
-            in_copies.append(copy)
+    make_tables(extent, extent // 2, wave, tables, zero)
+
     def keep(k, carry):
         fields[place * nb + k] = mine[place, k]
         return carry
@@ -591,29 +612,35 @@
         for i in range(1, group):
             tip_copy(i).wait_send()
 
-    for copy in in_copies:
-        copy.wait()
     in_edge_copy(0).wait_recv()
 
     @pl.when(last == 0)
     def _():
         tip_copy(1).wait_recv()
 
-    def wait_extra(m):
+    def wait_extra(u, m):
         @pl.when(place != 2 * m - 1)
         def _():
-            for u in range(len(rims)):
-                pltpu.make_async_remote_copy(
-                    src_ref=extra.at[0, pl.ds(u * unit, unit)],
-                    dst_ref=extra_held.at[pl.ds(m * yb + u * unit, unit)],
-                    send_sem=extra_send.at[u, 0],
-                    recv_sem=extra_recv.at[u, m],
-                    device_id={"space": beyond},
-                    device_id_type=MESH,
-                ).wait_recv()
-
-    for m in range(group // 2):
-        wait_extra(m)
+            pltpu.make_async_remote_copy(
+                src_ref=extra.at[0, pl.ds(u * unit, unit)],
+                dst_ref=extra_held.at[pl.ds(m * yb + u * unit, unit)],
+                send_sem=extra_send.at[u, 0],
+                recv_sem=extra_recv.at[u, m],
+                device_id={"space": beyond},
+                device_id_type=MESH,
+            ).wait_recv()
+
+    def wait_side(side):
+        for i in send_order(group):
+            parity = lax.rem(place + i + side, 2)
+            in_copy(parity, i).wait_recv()
+
+            @pl.when(parity == 0)
+            def _():
+                in_copy(jnp.int32(2), i).wait_recv()
+
+        for m in range(group // 2):
+            wait_extra(side, m)
 
     @pl.when(place == 0)
     def _():
@@ -649,16 +676,23 @@
         full = turn_in(c, [])
         return total + sum(full[8 * i : 8 * i + 8] * full[8 * i : 8 * i + 8] for i in range(lanes // 8))
 
-    theta = lax.fori_loop(0, columns, turn_rest, jnp.zeros((8, LANES), f32), unroll=3)
-    turn_in(0, [fields[planes * columns] + extra_held[group // 2 * yb]])
-    one[0:n, :] = pltpu.roll(one[0:n, :], LANES - 4, 1)
     def along_x(i, carry):
         parts = [one[rows_at(2 * i + e), :] for e in range(2)]
         for e, v in enumerate(transform(x_table[...], parts)):
             two[rows_at(2 * i + e), :] = v
         return carry
 
-    lax.fori_loop(0, n // 2, along_x, 0, unroll=4)
+    theta = jnp.zeros((8, LANES), f32)
+    for side in range(2):
+        wait_side(side)
+        theta = lax.fori_loop(side * unit, (side + 1) * unit, turn_rest, theta, unroll=3)
+        if side == 0:
+            turn_in(0, [fields[planes * columns] + extra_held[group // 2 * yb]])
+            one[0:n, :] = pltpu.roll(one[0:n, :], LANES - 4, 1)
+        lax.fori_loop(side * n // 4, (side + 1) * n // 4, along_x, 0, unroll=4)
+    for u in range(UNITS):
+        for i in range(1, group):
+            in_copy(u, i).wait_send()
 
     def along_z(i, carry):
         parts = [two[pl.ds(2 * i + e, n, stride=n), :] for e in range(2)]
@@ -799,7 +833,7 @@
     edges = [edge_copy(0, beyond), edge_copy(1, base + group - 1)]
 
     def each_unit(side, act):
-        for i in reversed(range(1, group)):
+        for i in send_order(group):
             parity = lax.rem(place + i, 2)
             if side == 0:
                 act(unit_copy(i, parity))
@@ -868,7 +902,7 @@
         return carry
 
     def arrive(v):
-        for i in reversed(range(1, group)):
+        for i in send_order(group):
             unit_copy(i, v).wait_recv()
 
         @pl.when(last * lax.div(v, UNITS) == 1)
@@ -933,20 +967,17 @@
     out_theta[...] = row[:, slices : slices + 1] * scales[0]
 
 
-def place_kernel(blocks, theta, deficit, out, out_theta, out_deficit, held_theta, held_deficit, small, sem):
+def place_kernel(blocks, theta, deficit, out, out_theta, out_deficit, small, sem):
     copies = [
         pltpu.make_async_copy(blocks.at[k], out.at[:, :, :, :, :, pl.ds(k * LANES, LANES)], sem.at[k])
         for k in range(blocks.shape[0])
     ]
+    copies = [
+        pltpu.make_async_copy(theta, out_theta, small.at[0]),
+        pltpu.make_async_copy(deficit, out_deficit, small.at[1]),
+    ] + copies
     for copy in copies:
         copy.start()
-    moves = [[(theta, held_theta), (held_theta, out_theta)], [(deficit, held_deficit), (held_deficit, out_deficit)]]
-    for leg in range(2):
-        short = [pltpu.make_async_copy(*move[leg], small.at[i]) for i, move in enumerate(moves)]
-        for copy in short:
-            copy.start()
-        for copy in short:
-            copy.wait()
     for copy in copies:
         copy.wait()
 
@@ -1017,9 +1048,9 @@
     new_links, total, shares = pl.pallas_call(
         place_kernel,
         out_shape=(shape(*links.shape), shape(1, 1), shape(1, slices)),
-        in_specs=[VM, ANY, ANY],
+        in_specs=[VM, VM, VM],
         out_specs=(ANY, ANY, ANY),
-        scratch_shapes=[vm(1, 1), vm(1, slices), dma(2), dma(nb)],
+        scratch_shapes=[dma(2), dma(nb)],
         compiler_params=pltpu.CompilerParams(vmem_limit_bytes=8 * 1024 * 1024),
     )(placed, total, shares)
     total = total.reshape(())

time: 67.2 us -> 65.4 us (0.973)
  Pallas kernels: 66.4 us -> 64.6 us
    pallas_call x1, Pallas kernels: 63.6 us -> 61.8 us  [call(): pl.pallas_call(kernel, out_shape=out_shape, in_specs=in_specs or [VM] * l...]
where the time goes in v6:
time: 65.4 us; the launch traced here: 65.2 us
  Pallas kernels  64.6 us (99%)
    pallas_call x1, Pallas kernels, call(): pl.pallas_call(kernel, out_shape=out_shape, in_specs=in_specs or [VM] * l...  61.8 us
    pallas_call x1, Pallas kernels, body(): pl.pallas_call(place_kernel, out_shape=(shape(*links.shape), shape(1, 1),...  2.82 us

profile of v6, /device:TPU:0, one launch (start us, length us, event | category | flops | bytes accessed | tf_op | source)
XLA Modules:
  0.0 65.2 jit_solution(7546636792778159708)
XLA Ops:
  0.6 61.8 %shard_map.38 = (f32[27,8,3,2,3,2,128]{6,5,4,3,2,1,0:T(2,128)S(1)}, f32[1,1]{1,0:T(1,128)}, f32[1,8]{1,0:T(1,128)S(1)}) custom-call(f32[8,3,2,3,2,3456]{5,4,3,2,1,0:T(2,128)} %links.1), custom_call_target="tpu_custom_call" | custom-call | flops 1000000000 | bytes 1000000 | tf_op jit(solution)/shard_map/pallas_call | solution.py:997
  62.4 2.8 %shard_map.39 = (f32[8,3,2,3,2,3456]{5,4,3,2,1,0:T(2,128)}, f32[1,1]{1,0:T(1,128)}, f32[1,8]{1,0:T(1,128)}) custom-call(f32[27,8,3,2,3,2,128]{6,5,4,3,2,1,0:T(2,128)S(1)} %get-tuple-element.9.blocks, f32[1,1]{1,0:T(1,128)} %get-tuple-element.10.theta, f32[1,8]{1,0:T(1,128)S(1)} %get-tuple-element.11.deficit), custom_call_target="tpu_custom_call" | custom-call | tf_op jit(solution)/shard_map/pallas_call | solution.py:1048

commit v7 on v6

--- a/solution.py
+++ b/solution.py
@@ -276,7 +276,7 @@
     ]
 
     def turn(v):
-        lax.fori_loop(v * unit, (v + 1) * unit, rotate_own, 0)
+        lax.fori_loop(0, unit, lambda i, carry: rotate_own(v * unit + i, carry), 0, unroll=3)
 
     def step(which, k, total):
         sl = block(k)
@@ -909,7 +909,7 @@
         def _():
             unit_copy(0, v).wait_recv()
 
-        lax.fori_loop(v * unit, (v + 1) * unit, gather, 0)
+        lax.fori_loop(0, unit, lambda i, carry: gather(v * unit + i, carry), 0, unroll=3)
 
     def mend_edges():
         @pl.when(place == 0)

time: 65.4 us -> 65.2 us (level)
  no operation moved by 1% of the time
where the time goes in v7:
time: 65.2 us; the launch traced here: 65.1 us
  Pallas kernels  64.4 us (99%)
    pallas_call x1, Pallas kernels, call(): pl.pallas_call(kernel, out_shape=out_shape, in_specs=in_specs or [VM] * l...  61.6 us
    pallas_call x1, Pallas kernels, body(): pl.pallas_call(place_kernel, out_shape=(shape(*links.shape), shape(1, 1),...  2.82 us

profile of v7, /device:TPU:0, one launch (start us, length us, event | category | flops | bytes accessed | tf_op | source)
XLA Modules:
  0.0 65.1 jit_solution(13611689816922604362)
XLA Ops:
  0.6 61.6 %shard_map.38 = (f32[27,8,3,2,3,2,128]{6,5,4,3,2,1,0:T(2,128)S(1)}, f32[1,1]{1,0:T(1,128)}, f32[1,8]{1,0:T(1,128)S(1)}) custom-call(f32[8,3,2,3,2,3456]{5,4,3,2,1,0:T(2,128)} %links.1), custom_call_target="tpu_custom_call" | custom-call | flops 1000000000 | bytes 1000000 | tf_op jit(solution)/shard_map/pallas_call | solution.py:997
  62.2 2.8 %shard_map.39 = (f32[8,3,2,3,2,3456]{5,4,3,2,1,0:T(2,128)}, f32[1,1]{1,0:T(1,128)}, f32[1,8]{1,0:T(1,128)}) custom-call(f32[27,8,3,2,3,2,128]{6,5,4,3,2,1,0:T(2,128)S(1)} %get-tuple-element.9.blocks, f32[1,1]{1,0:T(1,128)} %get-tuple-element.10.theta, f32[1,8]{1,0:T(1,128)S(1)} %get-tuple-element.11.deficit), custom_call_target="tpu_custom_call" | custom-call | tf_op jit(solution)/shard_map/pallas_call | solution.py:1048
